TPU v7x, 32 devices: a whole 2x2x4 slice. The times are simulated.
32 devices in a mesh: cells: 8 (over z, x), views: 4 (over y, core).
Axes of the slice: x: 2, y: 2, z: 4, core: 2. Of those that a mesh axis runs over, the one named last changes fastest.
Arguments:
- params: float32 [59, 16384], P(None, 'cells'), may hold values from -5 to 4, as said below
- first_moment: float32 [59, 16384], P(None, 'cells'), may hold values from -0.6 to 0.6
- second_moment: float32 [59, 16384], P(None, 'cells'), may hold values from 1e-12 to 0.05
- cameras: float32 [4, 6], P('views'), may hold values from -0.004 to 0.004
- visible: int32 [4, 16384], P('views', 'cells'), may hold values from 0 to 1, as said below
- send_plan: int32 [4, 8, 8, 256], P('views', 'cells'), may hold values from -1 to 2047, as said below
- tile_lists: int32 [4, 32, 512], P('views', 'cells'), may hold values from -1 to 2047, as said below
- target: float32 [4, 3, 8192], P('views', None, 'cells'), may hold values from 0 to 1
Outputs:
- updated_params: float32 [59, 16384], P(None, 'cells')
- updated_first: float32 [59, 16384], P(None, 'cells')
- updated_second: float32 [59, 16384], P(None, 'cells')
Inputs may be any that keep to these rules, and one draw needn't show every extreme that they name: `params`: rows 0 to 2 hold a Gaussian's mean, 3 to 5 the logarithms of its scales, 6 to 9 a rotation quaternion whose first component is at least 0.6, 10 its opacity logit, 11 to 58 its spherical-harmonic coefficients; every Gaussian lies at depth 2 or more before every camera. In each view, between a quarter and three quarters of each owner's block of 2048 Gaussians are visible. Every row of an owner's block of 2048 Gaussians belongs to exactly one rendering device, 256 rows to each device; send_plan[v, s, d, :] lists exactly the rows of owner s that belong to device d and are visible in view v, live entries first, then -1; in every view some device receives 256 rows from every owner. `tile_lists`: tile t is rendered on device t // 4; an entry e stands for send_plan[v, e // 256, t // 4, e % 256], which is live; live entries come first, ordered by increasing params[2] of their Gaussians, then -1; some tile of each view has 512 live entries.
All inputs are finite; a program needn't handle non-finite values.
Results may differ from a plain program's by a relative error of at most 0.0003.
Values sent between devices are 32-bit elements; how exact they have to be, the bound alone decides.
A program may use at most 64 MiB of HBM per device.

v0:
```python
import functools

import jax
import jax.numpy as jnp
from jax import lax
from jax.experimental import pallas as pl
from jax.experimental.pallas import tpu as pltpu
from jax.sharding import PartitionSpec as P

TILE_COLS = 32
ADAM_STEP = 1000


harmonic_zero = 0.28209479177387814
harmonic_one = 0.4886025119029199
harmonic_two = (
    1.0925484305920792,
    -1.0925484305920792,
    0.31539156525252005,
    -1.0925484305920792,
    0.5462742152960396,
)
harmonic_three = (
    -0.5900435899266435,
    2.890611442640554,
    -0.4570457994644658,
    0.3731763325901154,
    -0.4570457994644658,
    1.445305721320277,
    -0.5900435899266435,
)


def harmonics(across, upward, onward):
    across_sq = across * across
    upward_sq = upward * upward
    onward_sq = onward * onward
    return jnp.stack(
        [
            harmonic_zero * jnp.ones_like(across),
            -harmonic_one * upward,
            harmonic_one * onward,
            -harmonic_one * across,
            harmonic_two[0] * across * upward,
            harmonic_two[1] * upward * onward,
            harmonic_two[2] * (2.0 * onward_sq - across_sq - upward_sq),
            harmonic_two[3] * across * onward,
            harmonic_two[4] * (across_sq - upward_sq),
            harmonic_three[0] * upward * (3.0 * across_sq - upward_sq),
            harmonic_three[1] * across * upward * onward,
            harmonic_three[2] * upward * (4.0 * onward_sq - across_sq - upward_sq),
            harmonic_three[3] * onward * (2.0 * onward_sq - 3.0 * across_sq - 3.0 * upward_sq),
            harmonic_three[4] * across * (4.0 * onward_sq - across_sq - upward_sq),
            harmonic_three[5] * onward * (across_sq - upward_sq),
            harmonic_three[6] * across * (across_sq - 3.0 * upward_sq),
        ]
    )


def camera_rotation(angles):
    cos_roll, sin_roll = (jnp.cos(angles[0]), jnp.sin(angles[0]))
    cos_pitch, sin_pitch = (jnp.cos(angles[1]), jnp.sin(angles[1]))
    cos_yaw, sin_yaw = (jnp.cos(angles[2]), jnp.sin(angles[2]))
    naught = jnp.zeros_like(cos_roll)
    unit_one = jnp.ones_like(cos_roll)
    roll = jnp.stack(
        [
            jnp.stack([unit_one, naught, naught]),
            jnp.stack([naught, cos_roll, -sin_roll]),
            jnp.stack([naught, sin_roll, cos_roll]),
        ]
    )
    pitch = jnp.stack(
        [
            jnp.stack([cos_pitch, naught, sin_pitch]),
            jnp.stack([naught, unit_one, naught]),
            jnp.stack([-sin_pitch, naught, cos_pitch]),
        ]
    )
    yawing = jnp.stack(
        [
            jnp.stack([cos_yaw, -sin_yaw, naught]),
            jnp.stack([sin_yaw, cos_yaw, naught]),
            jnp.stack([naught, naught, unit_one]),
        ]
    )
    inner_turn = jnp.dot(pitch, roll, precision=lax.Precision.HIGHEST)
    return jnp.dot(yawing, inner_turn, precision=lax.Precision.HIGHEST)


def project(values, camera):
    turn = camera_rotation(camera[0:3])
    offset = values[0:3] - camera[3:6][:, None]
    in_view = jnp.dot(turn, offset, precision=lax.Precision.HIGHEST)
    inv_depth = 1.0 / in_view[2]
    screen_col = in_view[0] * inv_depth
    screen_row = in_view[1] * inv_depth
    scales = jnp.exp(values[3:6])
    quat = values[6:10] / jnp.sqrt(jnp.sum(values[6:10] * values[6:10], axis=0, keepdims=True))
    quat_w, quat_x, quat_y, quat_z = (quat[0], quat[1], quat[2], quat[3])
    spin = [
        [
            1.0 - 2.0 * (quat_y * quat_y + quat_z * quat_z),
            2.0 * (quat_x * quat_y - quat_w * quat_z),
            2.0 * (quat_x * quat_z + quat_w * quat_y),
        ],
        [
            2.0 * (quat_x * quat_y + quat_w * quat_z),
            1.0 - 2.0 * (quat_x * quat_x + quat_z * quat_z),
            2.0 * (quat_y * quat_z - quat_w * quat_x),
        ],
        [
            2.0 * (quat_x * quat_z - quat_w * quat_y),
            2.0 * (quat_y * quat_z + quat_w * quat_x),
            1.0 - 2.0 * (quat_x * quat_x + quat_y * quat_y),
        ],
    ]
    basis_cam = []
    for outer_index in range(3):
        row_terms = []
        for col_index in range(3):
            entry = turn[outer_index, 0] * spin[0][col_index]
            for mid_index in range(1, 3):
                entry = entry + turn[outer_index, mid_index] * spin[mid_index][col_index]
            row_terms.append(entry * scales[col_index])
        basis_cam.append(row_terms)
    jac_top = [
        (basis_cam[0][col_index] - screen_col * basis_cam[2][col_index]) * inv_depth
        for col_index in range(3)
    ]
    jac_low = [
        (basis_cam[1][col_index] - screen_row * basis_cam[2][col_index]) * inv_depth
        for col_index in range(3)
    ]
    sigma_a = jac_top[0] * jac_top[0] + jac_top[1] * jac_top[1] + jac_top[2] * jac_top[2]
    sigma_b = jac_top[0] * jac_low[0] + jac_top[1] * jac_low[1] + jac_top[2] * jac_low[2]
    sigma_c = jac_low[0] * jac_low[0] + jac_low[1] * jac_low[1] + jac_low[2] * jac_low[2]
    determinant = sigma_a * sigma_c - sigma_b * sigma_b
    opacity = jax.nn.sigmoid(values[10])
    distance = jnp.sqrt(jnp.sum(offset * offset, axis=0))
    unit_dir = offset / distance
    basis = harmonics(unit_dir[0], unit_dir[1], unit_dir[2])
    coeffs = values[11:59].reshape(16, 3, values.shape[1])
    colors = 0.5 + jnp.sum(basis[:, None, :] * coeffs, axis=0)
    screen = jnp.stack(
        [
            screen_col,
            screen_row,
            sigma_c / determinant,
            -sigma_b / determinant,
            sigma_a / determinant,
            opacity,
        ]
    )
    return jnp.concatenate([screen, colors], axis=0)


def group_loss(pieces):
    features, live_mask, pixel_column, pixel_row, target_tile = pieces
    entries = live_mask.shape[1]
    delta_col = pixel_column[:, :, None] - features[0][:, None, :]
    delta_row = pixel_row[:, :, None] - features[1][:, None, :]
    power = -0.5 * (
        features[2][:, None, :] * delta_col * delta_col
        + 2.0 * features[3][:, None, :] * delta_col * delta_row
        + features[4][:, None, :] * delta_row * delta_row
    )
    alphas = features[5][:, None, :] * jnp.exp(power) * live_mask[:, None, :]
    log_keep = jnp.log(1.0 - alphas)
    earlier = (
        lax.broadcasted_iota(jnp.int32, (entries, entries), 0)
        < lax.broadcasted_iota(jnp.int32, (entries, entries), 1)
    ).astype(jnp.float32)
    transmit = jnp.exp(
        jnp.einsum("bpl,lm->bpm", log_keep, earlier, precision=lax.Precision.HIGHEST)
    )
    weights = alphas * transmit
    image = jnp.einsum("bpl,kbl->kbp", weights, features[6:9], precision=lax.Precision.HIGHEST)
    error = image - target_tile
    return jnp.sum(error * error)


def render_tiles(picked, live_mask, pixel_column, pixel_row, target_tile):
    groups = live_mask.shape[0] // 4
    entries = live_mask.shape[1]
    pixels = pixel_column.shape[1]
    stacked = (
        jnp.transpose(picked.reshape(picked.shape[0], groups, 4, entries), (1, 0, 2, 3)),
        live_mask.reshape(groups, 4, entries),
        pixel_column.reshape(groups, 4, pixels),
        pixel_row.reshape(groups, 4, pixels),
        jnp.transpose(target_tile.reshape(3, groups, 4, pixels), (1, 0, 2, 3)),
    )
    return jnp.sum(lax.map(jax.checkpoint(group_loss), stacked))


def pixel_grid(first_tile, count, tiles_dev, rows_pix):
    tile_ids = first_tile + jnp.arange(count, dtype=jnp.int32)
    pixel_ids = jnp.arange(256, dtype=jnp.int32)
    block_cols = TILE_COLS // 4
    owner_ids = tile_ids // tiles_dev
    local_ids = tile_ids % tiles_dev
    tile_col = 4 * (owner_ids % block_cols) + local_ids % 4
    tile_row = tiles_dev // 4 * (owner_ids // block_cols) + local_ids // 4
    half_width = TILE_COLS * 8.0
    column = (tile_col[:, None] * 16 + pixel_ids[None, :] % 16).astype(jnp.float32)
    row_pos = (tile_row[:, None] * 16 + pixel_ids[None, :] // 16).astype(jnp.float32)
    return ((column + 0.5 - half_width) / half_width, (row_pos + 0.5 - rows_pix * 0.5) / half_width)


def adam_update(params, first_moment, second_moment, gradient, counts):
    row_ids = lax.broadcasted_iota(jnp.int32, params.shape, 0)
    rates = jnp.where(
        row_ids < 6,
        0.01,
        jnp.where(
            row_ids < 10,
            0.005,
            jnp.where(row_ids < 11, 0.05, jnp.where(row_ids < 14, 0.0025, 0.000125)),
        ),
    )
    first_new = 0.9 * first_moment + 0.1 * gradient
    second = 0.999 * second_moment + 0.001 * gradient * gradient
    bias_one = 1.0 - 0.9**ADAM_STEP
    bias_two = 1.0 - 0.999**ADAM_STEP
    stride = rates * (first_new / bias_one) / (jnp.sqrt(second / bias_two) + 1e-08)
    seen_mask = counts > 0.0
    return (
        jnp.where(seen_mask, params - stride, params),
        jnp.where(seen_mask, first_new, first_moment),
        jnp.where(seen_mask, second, second_moment),
    )


def shards(params, first_moment, second_moment, cameras, visible, send_plan, tile_lists, target):
    cells = lax.axis_size("cells")
    camera = cameras[0]
    plan_rows = send_plan[0, 0]
    capacity = plan_rows.shape[1]
    sent_live = (plan_rows >= 0)[None]
    sent_rows = jnp.maximum(plan_rows, 0)
    lists = tile_lists[0]
    tiles_here = lists.shape[0]
    live_mask = (lists >= 0).astype(jnp.float32)
    slot_ids = jnp.maximum(lists, 0)
    rows_pix = tiles_here * cells // TILE_COLS * 16
    pixel_column, pixel_row = pixel_grid(
        lax.axis_index("cells") * tiles_here, tiles_here, tiles_here, rows_pix
    )
    target_tile = target[0].reshape(3, tiles_here, 256)
    block = params.shape[1]

    def image_loss(table):
        picked = jnp.take(table, slot_ids, axis=1)
        return render_tiles(picked, live_mask, pixel_column, pixel_row, target_tile)

    def own_projection(values):
        return project(values, camera)

    features, project_pull = jax.vjp(own_projection, params)
    outgoing = jnp.take(features, sent_rows, axis=1)
    incoming = lax.all_to_all(outgoing, "cells", split_axis=1, concat_axis=1, tiled=True)
    loss_value, pullback = jax.vjp(
        image_loss, incoming.reshape(features.shape[0], cells * capacity)
    )
    table_grad = pullback(jnp.ones((), jnp.float32))[0]
    returned = lax.all_to_all(
        table_grad.reshape(features.shape[0], cells, capacity),
        "cells",
        split_axis=1,
        concat_axis=1,
        tiled=True,
    )
    kept = jnp.where(sent_live, returned, 0.0)
    gradient = project_pull(
        jnp.zeros((features.shape[0], block), jnp.float32).at[:, sent_rows].add(kept)
    )[0]
    seen_here = visible.astype(jnp.float32)
    total_grad, counts = lax.psum((gradient, seen_here), "views")
    new_params, new_first, new_second = adam_update(
        params, first_moment, second_moment, total_grad, counts
    )
    return (new_params, new_first, new_second)

LANES = 128
PAD_ROWS = 64
FEATS = 9


def project_rows(rows, turn, centre):
    offset = [rows[i] - centre[i] for i in range(3)]
    in_view = [
        turn[i][0] * offset[0] + turn[i][1] * offset[1] + turn[i][2] * offset[2] for i in range(3)
    ]
    inv_depth = 1.0 / in_view[2]
    screen_col = in_view[0] * inv_depth
    screen_row = in_view[1] * inv_depth
    scales = [jnp.exp(rows[3 + i]) for i in range(3)]
    raw = rows[6:10]
    norm = jnp.sqrt(raw[0] * raw[0] + raw[1] * raw[1] + raw[2] * raw[2] + raw[3] * raw[3])
    inv_norm = 1.0 / norm
    quat_w, quat_x, quat_y, quat_z = [item * inv_norm for item in raw]
    spin = [
        [
            1.0 - 2.0 * (quat_y * quat_y + quat_z * quat_z),
            2.0 * (quat_x * quat_y - quat_w * quat_z),
            2.0 * (quat_x * quat_z + quat_w * quat_y),
        ],
        [
            2.0 * (quat_x * quat_y + quat_w * quat_z),
            1.0 - 2.0 * (quat_x * quat_x + quat_z * quat_z),
            2.0 * (quat_y * quat_z - quat_w * quat_x),
        ],
        [
            2.0 * (quat_x * quat_z - quat_w * quat_y),
            2.0 * (quat_y * quat_z + quat_w * quat_x),
            1.0 - 2.0 * (quat_x * quat_x + quat_y * quat_y),
        ],
    ]
    basis_cam = [
        [
            (turn[i][0] * spin[0][j] + turn[i][1] * spin[1][j] + turn[i][2] * spin[2][j])
            * scales[j]
            for j in range(3)
        ]
        for i in range(3)
    ]
    top = [(basis_cam[0][j] - screen_col * basis_cam[2][j]) * inv_depth for j in range(3)]
    low = [(basis_cam[1][j] - screen_row * basis_cam[2][j]) * inv_depth for j in range(3)]
    sigma_a = top[0] * top[0] + top[1] * top[1] + top[2] * top[2]
    sigma_b = top[0] * low[0] + top[1] * low[1] + top[2] * low[2]
    sigma_c = low[0] * low[0] + low[1] * low[1] + low[2] * low[2]
    inv_det = 1.0 / (sigma_a * sigma_c - sigma_b * sigma_b)
    opacity = 1.0 / (1.0 + jnp.exp(-rows[10]))
    inv_dist = 1.0 / jnp.sqrt(offset[0] * offset[0] + offset[1] * offset[1] + offset[2] * offset[2])
    x, y, z = [item * inv_dist for item in offset]
    xx, yy, zz = x * x, y * y, z * z
    basis = [
        None,
        -harmonic_one * y,
        harmonic_one * z,
        -harmonic_one * x,
        harmonic_two[0] * x * y,
        harmonic_two[1] * y * z,
        harmonic_two[2] * (2.0 * zz - xx - yy),
        harmonic_two[3] * x * z,
        harmonic_two[4] * (xx - yy),
        harmonic_three[0] * y * (3.0 * xx - yy),
        harmonic_three[1] * x * y * z,
        harmonic_three[2] * y * (4.0 * zz - xx - yy),
        harmonic_three[3] * z * (2.0 * zz - 3.0 * xx - 3.0 * yy),
        harmonic_three[4] * x * (4.0 * zz - xx - yy),
        harmonic_three[5] * z * (xx - yy),
        harmonic_three[6] * x * (xx - 3.0 * yy),
    ]
    colors = []
    for k in range(3):
        total = harmonic_zero * rows[11 + k]
        for j in range(1, 16):
            total = total + basis[j] * rows[11 + 3 * j + k]
        colors.append(0.5 + total)
    return (
        screen_col,
        screen_row,
        sigma_c * inv_det,
        -sigma_b * inv_det,
        sigma_a * inv_det,
        opacity,
        *colors,
    )


def camera_terms(cam):
    cosines, sines = jnp.cos(cam), jnp.sin(cam)
    cr, cp, cy = [cosines[:, i : i + 1] for i in range(3)]
    sr, sp, sy = [sines[:, i : i + 1] for i in range(3)]
    turn = [
        [cy * cp, cy * sp * sr - sy * cr, cy * sp * cr + sy * sr],
        [sy * cp, sy * sp * sr + cy * cr, sy * sp * cr - cy * sr],
        [-sp, cp * sr, cp * cr],
    ]
    centre = [cam[:, 3 + i : 4 + i] for i in range(3)]
    return turn, centre


def stage_rows(params_ref, staged):
    count, block = params_ref.shape
    for b in range(block // LANES):
        staged[b * PAD_ROWS : b * PAD_ROWS + count, :] = params_ref[:, b * LANES : (b + 1) * LANES]


def lane_pick(source, lanes):
    return jnp.take_along_axis(source, lanes, axis=1, mode="promise_in_bounds")


def gather_eight(load, blocks, index):
    index = jnp.maximum(index, 0)
    lanes, block = index & (LANES - 1), index >> 7
    total = lane_pick(load(0), lanes)
    for b in range(1, blocks):
        total = jnp.where(block == b, lane_pick(load(b), lanes), total)
    return total


def split_three(x):
    first = x.astype(jnp.bfloat16).astype(jnp.float32)
    rest = x - first
    second = rest.astype(jnp.bfloat16).astype(jnp.float32)
    return first, second, rest - second


def scatter_fill(g, index, lhs, hot, start):
    width = g.shape[1]
    parts = jnp.concatenate(split_three(g), axis=0)
    high, low = index >> 7, index & (LANES - 1)
    blocks = lhs.shape[0] // parts.shape[0]
    size = parts.shape[0]
    for b in range(blocks):
        lhs[b * size : (b + 1) * size, pl.ds(start, width)] = jnp.where(
            high == b, parts, 0.0
        ).astype(jnp.bfloat16)
    lane_ids = lax.broadcasted_iota(jnp.int32, (LANES, width), 0)
    hot[:, pl.ds(start, width)] = jnp.where(lane_ids == low, 1.0, 0.0).astype(jnp.bfloat16)


def scatter_finish(lhs, hot):
    out = lax.dot_general(
        lhs[...], hot[...], (((1,), (1,)), ((), ())), preferred_element_type=jnp.float32
    )
    blocks = lhs.shape[0] // 48
    return [
        out[48 * b : 48 * b + 16] + out[48 * b + 16 : 48 * b + 32] + out[48 * b + 32 : 48 * b + 48]
        for b in range(blocks)
    ]


def project_kernel(params_ref, cam_ref, plan_ref, out_ref, staged, table, last, order):
    count, block = params_ref.shape
    blocks = block // LANES
    halves = plan_ref.shape[1] // LANES
    stage_rows(params_ref, staged)
    turn, centre = camera_terms(cam_ref[...])
    for part in range(blocks // 8):
        base = part * 8 * PAD_ROWS
        rows = [staged[pl.ds(base + r, 8, stride=PAD_ROWS), :] for r in range(count)]
        feats = project_rows(rows, turn, centre)
        for f in range(8):
            table[pl.ds(part * 64 + f, 8, stride=8), :] = feats[f]
        last[part * 8 : part * 8 + 8, :] = feats[8]
    slots = plan_ref.shape[0] * halves
    for o in range(slots):
        d, h = divmod(o, halves)
        row = plan_ref[d : d + 1, h * LANES : (h + 1) * LANES]
        order[o : o + 1, :] = row
        out_ref[d, 8 * h : 8 * h + 8, :] = gather_eight(
            lambda b: table[8 * b : 8 * b + 8, :], blocks, jnp.broadcast_to(row, (8, LANES))
        )
    for p in range(slots // 8):
        picked = gather_eight(
            lambda b: jnp.broadcast_to(last[b : b + 1, :], (8, LANES)),
            blocks,
            order[8 * p : 8 * p + 8, :],
        )
        for i in range(8 // halves):
            out_ref[8 // halves * p + i, 8 * halves :, :] = picked[i * halves : (i + 1) * halves]


def exchange_kernel(axis, size, spread, src_ref, dst_ref, send_sem, recv_sem, own_sem):
    me = lax.axis_index(axis)
    barrier = pltpu.get_barrier_semaphore()
    for k in range(1, size):
        pl.semaphore_signal(
            barrier,
            inc=1,
            device_id={axis: lax.rem(me + k, size)},
            device_id_type=pl.DeviceIdType.MESH,
        )
    mine = pltpu.make_async_copy(src_ref.at[me] if spread else src_ref, dst_ref.at[me], own_sem)
    mine.start()
    pl.semaphore_wait(barrier, size - 1)
    copies = []
    for k in range(1, size):
        peer = lax.rem(me + k, size)
        copy = pltpu.make_async_remote_copy(
            src_ref=src_ref.at[peer] if spread else src_ref,
            dst_ref=dst_ref.at[me],
            send_sem=send_sem.at[k - 1],
            recv_sem=recv_sem.at[k - 1],
            device_id={axis: peer},
            device_id_type=pl.DeviceIdType.MESH,
        )
        copy.start()
        copies.append(copy)
    mine.wait()
    for copy in copies:
        copy.wait()


def exchange(x, axis, spread, collective):
    size = lax.axis_size(axis)
    shape = x.shape if spread else (size,) + x.shape
    return pl.pallas_call(
        functools.partial(exchange_kernel, axis, size, spread),
        out_shape=jax.ShapeDtypeStruct(shape, x.dtype),
        in_specs=[pl.BlockSpec(memory_space=pltpu.VMEM)],
        out_specs=pl.BlockSpec(memory_space=pltpu.VMEM),
        scratch_shapes=[
            pltpu.SemaphoreType.DMA((size - 1,)),
            pltpu.SemaphoreType.DMA((size - 1,)),
            pltpu.SemaphoreType.DMA,
        ],
        compiler_params=pltpu.CompilerParams(collective_id=collective, has_side_effects=True),
    )(x)


def render_kernel(
    cells, recv_ref, lists_ref, target_ref, out_ref,
    order, picks, wanted, before, after, alpha_s, trans_s, flow_s, parts_s, pair_s, lhs, hot,
):
    tiles, entries = lists_ref.shape
    owners, packed, _ = recv_ref.shape
    halves = packed // FEATS
    blocks = owners * halves
    quarters = entries // LANES
    me = lax.axis_index("cells")
    rows_pix = tiles * cells // TILE_COLS * 16
    half_width = TILE_COLS * 8.0
    wanted[...] = jnp.transpose(
        jnp.concatenate([target_ref[...], jnp.zeros((5, target_ref.shape[1]), jnp.float32)], axis=0)
    )
    row_ids = lax.broadcasted_iota(jnp.int32, (entries, entries), 0)
    col_ids = lax.broadcasted_iota(jnp.int32, (entries, entries), 1)
    before[...] = jnp.where(row_ids < col_ids, 1.0, 0.0).astype(jnp.bfloat16)
    after[...] = jnp.where(row_ids > col_ids, 1.0, 0.0).astype(jnp.bfloat16)

    def load_main(b):
        s, h = divmod(b, halves)
        return recv_ref[s, 8 * h : 8 * h + 8, :]

    def load_last(b):
        s, h = divmod(b, halves)
        return jnp.broadcast_to(recv_ref[s, 8 * halves + h : 8 * halves + h + 1, :], (8, LANES))

    slots = tiles * quarters
    for o in range(slots):
        t, q = divmod(o, quarters)
        row = lists_ref[t : t + 1, q * LANES : (q + 1) * LANES]
        order[o : o + 1, :] = row
        picks[t, 0:8, q * LANES : (q + 1) * LANES] = gather_eight(
            load_main, blocks, jnp.broadcast_to(row, (8, LANES))
        )
    for p in range(slots // 8):
        picked = gather_eight(load_last, blocks, order[8 * p : 8 * p + 8, :])
        for i in range(8):
            t, q = divmod(8 * p + i, quarters)
            picks[t, 8:9, q * LANES : (q + 1) * LANES] = picked[i : i + 1]

    def one_tile(t, carry):
        def feature(f):
            return picks[t, f : f + 1, :]

        listed = lists_ref[pl.ds(t, 1), :]
        opacity = jnp.where(listed >= 0, feature(5), 0.0)
        tile_col = 4 * lax.rem(me, TILE_COLS // 4) + lax.rem(t, 4)
        tile_row = tiles // 4 * lax.div(me, TILE_COLS // 4) + lax.div(t, 4)
        across = (lax.broadcasted_iota(jnp.int32, (16, entries), 0) + tile_col * 16).astype(jnp.float32)
        delta_col = (across + 0.5 - half_width) * (1.0 / half_width) - feature(0)
        square_term = -0.5 * feature(2) * delta_col * delta_col
        cross_term = -feature(3) * delta_col
        row_scale = -0.5 * feature(4)

        def delta_row_at(r):
            down = (jnp.full((1, entries), tile_row * 16 + r, jnp.int32)).astype(jnp.float32)
            return (down + 0.5 - rows_pix * 0.5) * (1.0 / half_width) - feature(1)

        def put_parts(r, x):
            first = x.astype(jnp.bfloat16)
            parts_s[pl.ds(r * 16, 16), :] = first
            parts_s[pl.ds(256 + r * 16, 16), :] = (x - first.astype(jnp.float32)).astype(jnp.bfloat16)

        def forward(r, carry):
            delta_row = delta_row_at(r)
            power = square_term + cross_term * delta_row + row_scale * delta_row * delta_row
            alpha = opacity * jnp.exp(power)
            alpha_s[pl.ds(r * 16, 16), :] = alpha
            put_parts(r, jnp.log(1.0 - alpha))
            return carry

        lax.fori_loop(0, 16, forward, 0, unroll=4)
        sums = jnp.dot(parts_s[...], before[...], preferred_element_type=jnp.float32)
        trans_s[...] = jnp.exp(sums[0:256] + sums[256:512])

        def errors_of(r, carry):
            weight = alpha_s[pl.ds(r * 16, 16), :] * trans_s[pl.ds(r * 16, 16), :]
            where = pl.ds(t * 256 + r * 16, 16)
            values = [jnp.sum(weight * feature(6 + k), axis=1, keepdims=True) for k in range(3)]
            lane = lax.broadcasted_iota(jnp.int32, (16, 8), 1)
            image = jnp.where(lane == 0, values[0], jnp.where(lane == 1, values[1], values[2]))
            wanted[where, :] = 2.0 * (image - wanted[where, :])
            return carry

        lax.fori_loop(0, 16, errors_of, 0, unroll=8)

        def colors_of(r, carry):
            weight = alpha_s[pl.ds(r * 16, 16), :] * trans_s[pl.ds(r * 16, 16), :]
            errors = wanted[pl.ds(t * 256 + r * 16, 16), :]
            slope = 0.0
            sums = []
            for k in range(3):
                error = errors[:, k : k + 1]
                slope = slope + error * feature(6 + k)
                sums.append(carry[k] + error * weight)
            flow = weight * slope
            flow_s[pl.ds(r * 16, 16), :] = flow
            put_parts(r, flow)
            return tuple(sums)

        empty = jnp.zeros((16, entries), jnp.float32)
        color_sums = lax.fori_loop(0, 16, colors_of, (empty, empty, empty), unroll=4)
        sums = jnp.dot(parts_s[...], after[...], preferred_element_type=jnp.float32)
        trans_s[...] = sums[0:256] + sums[256:512]

        def backward(r, carry):
            delta_row = delta_row_at(r)
            alpha = alpha_s[pl.ds(r * 16, 16), :]
            slope = flow_s[pl.ds(r * 16, 16), :] - alpha / (1.0 - alpha) * trans_s[pl.ds(r * 16, 16), :]
            return (
                carry[0] + slope,
                carry[1] + slope * delta_row,
                carry[2] + slope * (delta_row * delta_row),
            )

        plain, tilted, bent = lax.fori_loop(0, 16, backward, (empty, empty, empty), unroll=4)

        def fold(x):
            return jnp.sum(x, axis=0, keepdims=True)

        moved = plain * delta_col
        pair_s[...] = jnp.concatenate(
            [
                fold(plain),
                fold(moved),
                fold(tilted),
                fold(moved * delta_col),
                fold(tilted * delta_col),
                fold(bent),
                fold(color_sums[0]),
                fold(color_sums[1]),
                fold(color_sums[2]),
                jnp.zeros((7, entries), jnp.float32),
            ],
            axis=0,
        )
        scatter_fill(pair_s[...], listed, lhs, hot, pl.multiple_of(t * entries, entries))
        return carry

    lax.fori_loop(0, tiles, one_tile, 0)
    for b, piece in enumerate(scatter_finish(lhs, hot)):
        s, h = divmod(b, halves)
        out_ref[s, 8 * h : 8 * h + 8, :] = piece[0:8]
        out_ref[s, 8 * halves + h : 8 * halves + h + 1, :] = piece[8:9]


def owner_kernel(back_ref, plan_ref, visible_ref, cam_ref, out_ref, lhs, hot, spread):
    devices, packed, _ = back_ref.shape
    halves = packed // FEATS
    for d in range(devices):
        main = jnp.concatenate([back_ref[d, 8 * h : 8 * h + 8, :] for h in range(halves)], axis=1)
        last = jnp.concatenate(
            [back_ref[d, 8 * halves + h : 8 * halves + h + 1, :] for h in range(halves)], axis=1
        )
        g = jnp.concatenate([main, last, jnp.zeros((7, halves * LANES), jnp.float32)], axis=0)
        scatter_fill(g, plan_ref[d : d + 1, :], lhs, hot, d * halves * LANES)
    pieces = scatter_finish(lhs, hot)
    blocks = len(pieces)
    for b, piece in enumerate(pieces):
        spread[16 * b : 16 * b + 16, :] = piece
    for f in range(FEATS):
        out_ref[f] = spread[pl.ds(f, blocks, stride=16), :]
    for b in range(blocks):
        out_ref[FEATS, b : b + 1, :] = visible_ref[:, b * LANES : (b + 1) * LANES].astype(jnp.float32)
    out_ref[FEATS + 1] = jnp.broadcast_to(
        jnp.concatenate([cam_ref[...], jnp.zeros((1, LANES - 6), jnp.float32)], axis=1),
        (blocks, LANES),
    )


def update_kernel(params_ref, first_ref, second_ref, shared_ref, new_ref, new_first_ref, new_second_ref, staged, grads):
    count, block = params_ref.shape
    blocks = block // LANES
    views = shared_ref.shape[0]
    stage_rows(params_ref, staged)
    grads[...] = jnp.zeros_like(grads)

    def one_part(step, carry):
        part, view = lax.div(step, views), lax.rem(step, views)
        base = part * (8 * PAD_ROWS)
        start = pl.multiple_of(part * 8, 8)
        cam = shared_ref[view, FEATS + 1, 0:1, :]
        turn, centre = camera_terms(cam)
        rows = tuple(staged[pl.ds(base + r, 8, stride=PAD_ROWS), :] for r in range(count))
        feats, pull = jax.vjp(lambda *items: project_rows(items, turn, centre), *rows)
        got = [shared_ref[view, f, pl.ds(start, 8), :] for f in range(FEATS)]
        slopes = (
            feats[2] * got[1] + feats[3] * got[2],
            feats[3] * got[1] + feats[4] * got[2],
            -0.5 * got[3],
            -got[4],
            -0.5 * got[5],
            got[0] / feats[5],
            got[6],
            got[7],
            got[8],
        )
        for r, item in enumerate(pull(slopes)):
            where = pl.ds(base + r, 8, stride=PAD_ROWS)
            grads[where, :] = grads[where, :] + item
        return carry

    lax.fori_loop(0, blocks // 8 * views, one_part, 0)
    row_ids = lax.broadcasted_iota(jnp.int32, (count, LANES), 0)
    rates = jnp.where(
        row_ids < 6,
        0.01,
        jnp.where(
            row_ids < 10,
            0.005,
            jnp.where(row_ids < 11, 0.05, jnp.where(row_ids < 14, 0.0025, 0.000125)),
        ),
    )
    bias_one = 1.0 - 0.9**ADAM_STEP
    bias_two = 1.0 - 0.999**ADAM_STEP
    for b in range(blocks):
        span = slice(b * LANES, (b + 1) * LANES)
        gradient = grads[b * PAD_ROWS : b * PAD_ROWS + count, :]
        params, first, second = params_ref[:, span], first_ref[:, span], second_ref[:, span]
        counts = shared_ref[0, FEATS, b : b + 1, :]
        for view in range(1, views):
            counts = counts + shared_ref[view, FEATS, b : b + 1, :]
        seen = jnp.broadcast_to(counts, params.shape) > 0.0
        first_new = 0.9 * first + 0.1 * gradient
        second_new = 0.999 * second + 0.001 * gradient * gradient
        stride = rates * (first_new / bias_one) / (jnp.sqrt(second_new / bias_two) + 1e-08)
        new_ref[:, span] = jnp.where(seen, params - stride, params)
        new_first_ref[:, span] = jnp.where(seen, first_new, first)
        new_second_ref[:, span] = jnp.where(seen, second_new, second)


def fused_shards(params, first_moment, second_moment, cameras, visible, send_plan, tile_lists, target):
    cells = lax.axis_size("cells")
    count, block = params.shape
    blocks = block // LANES
    plan = send_plan[0, 0]
    lists = tile_lists[0]
    tiles, entries = lists.shape
    halves = plan.shape[1] // LANES
    slots = cells * halves
    f32, bf16 = jnp.float32, jnp.bfloat16
    packet = jax.ShapeDtypeStruct((cells, FEATS * halves, LANES), f32)
    outgoing = pl.pallas_call(
        project_kernel,
        out_shape=packet,
        scratch_shapes=[
            pltpu.VMEM((blocks * PAD_ROWS, LANES), f32),
            pltpu.VMEM((blocks * 8, LANES), f32),
            pltpu.VMEM((blocks, LANES), f32),
            pltpu.VMEM((slots, LANES), jnp.int32),
        ],
    )(params, cameras, plan)
    incoming = exchange(outgoing, "cells", True, 0)
    back = pl.pallas_call(
        functools.partial(render_kernel, cells),
        out_shape=packet,
        scratch_shapes=[
            pltpu.VMEM((tiles * entries // LANES, LANES), jnp.int32),
            pltpu.VMEM((tiles, 16, entries), f32),
            pltpu.VMEM((tiles * 256, 8), f32),
            pltpu.VMEM((entries, entries), bf16),
            pltpu.VMEM((entries, entries), bf16),
            pltpu.VMEM((256, entries), f32),
            pltpu.VMEM((256, entries), f32),
            pltpu.VMEM((256, entries), f32),
            pltpu.VMEM((512, entries), bf16),
            pltpu.VMEM((16, entries), f32),
            pltpu.VMEM((slots * 48, tiles * entries), bf16),
            pltpu.VMEM((LANES, tiles * entries), bf16),
        ],
    )(incoming, lists, target[0])
    returned = exchange(back, "cells", True, 1)
    mine = pl.pallas_call(
        owner_kernel,
        out_shape=jax.ShapeDtypeStruct((FEATS + 2, blocks, LANES), f32),
        scratch_shapes=[
            pltpu.VMEM((blocks * 48, slots * LANES), bf16),
            pltpu.VMEM((LANES, slots * LANES), bf16),
            pltpu.VMEM((blocks * 16, LANES), f32),
        ],
    )(returned, plan, visible, cameras)
    shared = exchange(mine, "views", False, 2)
    like = jax.ShapeDtypeStruct(params.shape, f32)
    return tuple(
        pl.pallas_call(
            update_kernel,
            out_shape=(like, like, like),
            scratch_shapes=[
                pltpu.VMEM((blocks * PAD_ROWS, LANES), f32),
                pltpu.VMEM((blocks * PAD_ROWS, LANES), f32),
            ],
        )(params, first_moment, second_moment, shared)
    )


def local_shards(params, first_moment, second_moment, cameras, visible, send_plan, tile_lists, target):
    capacity = send_plan.shape[3]
    tiles, entries = tile_lists.shape[1:]
    halves = capacity // LANES
    fits = (
        capacity % LANES == 0
        and params.shape[1] % (8 * LANES) == 0
        and entries % LANES == 0
        and 8 % max(halves, 1) == 0
        and lax.axis_size("cells") * halves % 8 == 0
        and tiles * entries // LANES % 8 == 0
        and tiles * entries <= 4096
        and tiles % 4 == 0
    )
    body = fused_shards if fits else shards
    return body(params, first_moment, second_moment, cameras, visible, send_plan, tile_lists, target)


def solution(mesh):
    in_specs = (
        P(None, "cells"),
        P(None, "cells"),
        P(None, "cells"),
        P("views", None),
        P("views", "cells"),
        P("views", "cells", None, None),
        P("views", "cells", None),
        P("views", None, "cells"),
    )
    out_specs = (P(None, "cells"), P(None, "cells"), P(None, "cells"))
    return jax.shard_map(local_shards, mesh=mesh, in_specs=in_specs, out_specs=out_specs, check_vma=False)
```

profile of v0, /device:TPU:1, one launch (start us, length us, event | category | flops | bytes accessed | tf_op | source)
XLA Modules:
  0.0 55.3 jit_solution(12833509743477339007)
XLA Ops:
  0.6 1.3 %copy.13 = f32[1,3,1024]{2,1,0:T(4,128)} copy(f32[1,3,1024]{2,0,1:T(1,128)} %param.15) | data formatting | bytes 24576
  1.9 2.5 %shard_map.103.src_ref = f32[8,18,128]{2,1,0:T(8,128)} custom-call(f32[59,2048]{1,0:T(8,128)} %params_ref.3, f32[1,6]{1,0:T(1,128)} %cam_ref.3, s32[8,256]{1,0:T(8,128)} %bitcast.6), custom_call_target="tpu_custom_call" | custom-call | tf_op jit(solution)/shard_map/pallas_call | solution.py:760
  4.5 8.7 %shard_map.104.recv_ref = f32[8,18,128]{2,1,0:T(8,128)} custom-call(f32[8,18,128]{2,1,0:T(8,128)} %shard_map.103.src_ref), custom_call_target="tpu_custom_call" | custom-call | tf_op jit(solution)/shard_map/pallas_call | solution.py:502
  13.2 13.7 %shard_map.105.src_ref = f32[8,18,128]{2,1,0:T(8,128)} custom-call(f32[8,18,128]{2,1,0:T(8,128)} %shard_map.104.recv_ref, s32[4,512]{1,0:T(4,128)} %bitcast.8, f32[3,1024]{1,0:T(4,128)} %bitcast.5), custom_call_target="tpu_custom_call" | custom-call | tf_op jit(solution)/shard_map/pallas_call | solution.py:771
  26.9 7.1 %shard_map.106.back_ref = f32[8,18,128]{2,1,0:T(8,128)} custom-call(f32[8,18,128]{2,1,0:T(8,128)} %shard_map.105.src_ref), custom_call_target="tpu_custom_call" | custom-call | tf_op jit(solution)/shard_map/pallas_call | solution.py:502
  34.0 2.9 %shard_map.107.src_ref = f32[11,16,128]{2,1,0:T(8,128)} custom-call(f32[8,18,128]{2,1,0:T(8,128)} %shard_map.106.back_ref, s32[8,256]{1,0:T(8,128)} %bitcast.7, s32[1,2048]{1,0:T(1,128)} %visible_ref.1, f32[1,6]{1,0:T(1,128)} %cam_ref.3), custom_call_target="tpu_custom_call" | custom-call | tf_op jit(solution)/shard_map/pallas_call | solution.py:790
  36.8 10.7 %shard_map.108.shared_ref = f32[4,11,16,128]{3,2,1,0:T(8,128)} custom-call(f32[11,16,128]{2,1,0:T(8,128)} %shard_map.107.src_ref), custom_call_target="tpu_custom_call" | custom-call | tf_op jit(solution)/shard_map/pallas_call | solution.py:502
  47.5 7.8 %shard_map.109 = (f32[59,2048]{1,0:T(8,128)}, f32[59,2048]{1,0:T(8,128)}, f32[59,2048]{1,0:T(8,128)}) custom-call(f32[59,2048]{1,0:T(8,128)} %params_ref.3, f32[59,2048]{1,0:T(8,128)} %first_ref.1, f32[59,2048]{1,0:T(8,128)} %second_ref.1, f32[4,11,16,128]{3,2,1,0:T(8,128)} %shard_map.108.shared_ref), custom_call_target="tpu_custom_call" | custom-call | tf_op jit(solution)/shard_map/pallas_call | solution.py:802
where the time goes:
time: 55.7 us; the launch traced here: 55.3 us
  Pallas kernels  53.3 us (96%)
  local copies, waits for them, and re-layouts  1.32 us (2%)
  between operations  0.66 us (1%)
    pallas_call x3, Pallas kernels, exchange(): pl.pallas_call(functools.partial(exchange_kernel, axis, size, spread), ou...  26.5 us
    pallas_call x1, Pallas kernels, fused_shards(): pl.pallas_call(functools.partial(render_kernel, cells), out_shape=packet,...  13.7 us
    pallas_call x1, Pallas kernels, fused_shards(): pl.pallas_call(update_kernel, out_shape=(like, like, like), scratch_shape...  7.77 us
    pallas_call x1, Pallas kernels, fused_shards(): pl.pallas_call(owner_kernel, out_shape=jax.ShapeDtypeStruct((FEATS + 2, b...  2.86 us
    pallas_call x1, Pallas kernels, fused_shards(): pl.pallas_call(project_kernel, out_shape=packet, scratch_shapes=[pltpu.VM...  2.51 us
    unnamed x1, local copies, waits for them, and re-layouts  1.32 us

commit v1 on v0

--- a/solution.py
+++ b/solution.py
@@ -465,54 +465,6 @@
             out_ref[8 // halves * p + i, 8 * halves :, :] = picked[i * halves : (i + 1) * halves]
 
 
-def exchange_kernel(axis, size, spread, src_ref, dst_ref, send_sem, recv_sem, own_sem):
-    me = lax.axis_index(axis)
-    barrier = pltpu.get_barrier_semaphore()
-    for k in range(1, size):
-        pl.semaphore_signal(
-            barrier,
-            inc=1,
-            device_id={axis: lax.rem(me + k, size)},
-            device_id_type=pl.DeviceIdType.MESH,
-        )
-    mine = pltpu.make_async_copy(src_ref.at[me] if spread else src_ref, dst_ref.at[me], own_sem)
-    mine.start()
-    pl.semaphore_wait(barrier, size - 1)
-    copies = []
-    for k in range(1, size):
-        peer = lax.rem(me + k, size)
-        copy = pltpu.make_async_remote_copy(
-            src_ref=src_ref.at[peer] if spread else src_ref,
-            dst_ref=dst_ref.at[me],
-            send_sem=send_sem.at[k - 1],
-            recv_sem=recv_sem.at[k - 1],
-            device_id={axis: peer},
-            device_id_type=pl.DeviceIdType.MESH,
-        )
-        copy.start()
-        copies.append(copy)
-    mine.wait()
-    for copy in copies:
-        copy.wait()
-
-
-def exchange(x, axis, spread, collective):
-    size = lax.axis_size(axis)
-    shape = x.shape if spread else (size,) + x.shape
-    return pl.pallas_call(
-        functools.partial(exchange_kernel, axis, size, spread),
-        out_shape=jax.ShapeDtypeStruct(shape, x.dtype),
-        in_specs=[pl.BlockSpec(memory_space=pltpu.VMEM)],
-        out_specs=pl.BlockSpec(memory_space=pltpu.VMEM),
-        scratch_shapes=[
-            pltpu.SemaphoreType.DMA((size - 1,)),
-            pltpu.SemaphoreType.DMA((size - 1,)),
-            pltpu.SemaphoreType.DMA,
-        ],
-        compiler_params=pltpu.CompilerParams(collective_id=collective, has_side_effects=True),
-    )(x)
-
-
 def render_kernel(
     cells, recv_ref, lists_ref, target_ref, out_ref,
     order, picks, wanted, before, after, alpha_s, trans_s, flow_s, parts_s, pair_s, lhs, hot,
@@ -526,7 +478,10 @@
     rows_pix = tiles * cells // TILE_COLS * 16
     half_width = TILE_COLS * 8.0
     wanted[...] = jnp.transpose(
-        jnp.concatenate([target_ref[...], jnp.zeros((5, target_ref.shape[1]), jnp.float32)], axis=0)
+        jnp.concatenate(
+            [target_ref[k] for k in range(3)] + [jnp.zeros((5, target_ref.shape[2]), jnp.float32)],
+            axis=0,
+        )
     )
     row_ids = lax.broadcasted_iota(jnp.int32, (entries, entries), 0)
     col_ids = lax.broadcasted_iota(jnp.int32, (entries, entries), 1)
@@ -661,7 +616,7 @@
         out_ref[s, 8 * halves + h : 8 * halves + h + 1, :] = piece[8:9]
 
 
-def owner_kernel(back_ref, plan_ref, visible_ref, cam_ref, out_ref, lhs, hot, spread):
+def owner_rows(back_ref, plan_ref, out_ref, lhs, hot, spread):
     devices, packed, _ = back_ref.shape
     halves = packed // FEATS
     for d in range(devices):
@@ -676,13 +631,100 @@
     for b, piece in enumerate(pieces):
         spread[16 * b : 16 * b + 16, :] = piece
     for f in range(FEATS):
-        out_ref[f] = spread[pl.ds(f, blocks, stride=16), :]
+        out_ref[f * blocks : (f + 1) * blocks, :] = spread[pl.ds(f, blocks, stride=16), :]
+
+
+def main_kernel(
+    params_ref, cam_ref, plan_ref, visible_ref, lists_ref, target_ref, shared_ref,
+    staged, table, last, plan_order, outgoing, incoming, back, returned, mine, extra,
+    order, picks, wanted, before, after, alpha_s, trans_s, flow_s, parts_s, pair_s, lhs, hot,
+    own_lhs, own_hot, spread,
+    send_one, recv_one, send_two, recv_two, send_three, recv_three, send_four, recv_four, local_sem,
+):
+    cells, views = lax.axis_size("cells"), lax.axis_size("views")
+    cell, view = lax.axis_index("cells"), lax.axis_index("views")
+    blocks = params_ref.shape[1] // LANES
+    grads = FEATS * blocks
+    barrier = pltpu.get_barrier_semaphore()
+
+    def greet(axis, me, size):
+        for k in range(1, size):
+            pl.semaphore_signal(
+                barrier,
+                inc=1,
+                device_id={axis: lax.rem(me + k, size)},
+                device_id_type=pl.DeviceIdType.MESH,
+            )
+
+    def send_all(axis, me, size, source, dest, send_sem, recv_sem):
+        copies = []
+        for k in range(1, size):
+            peer = lax.rem(me + k, size)
+            copy = pltpu.make_async_remote_copy(
+                src_ref=source(peer),
+                dst_ref=dest(me),
+                send_sem=send_sem.at[k - 1],
+                recv_sem=recv_sem.at[k - 1],
+                device_id={axis: peer},
+                device_id_type=pl.DeviceIdType.MESH,
+            )
+            copy.start()
+            copies.append(copy)
+        return copies
+
+    greet("cells", cell, cells)
+    greet("views", view, views)
     for b in range(blocks):
-        out_ref[FEATS, b : b + 1, :] = visible_ref[:, b * LANES : (b + 1) * LANES].astype(jnp.float32)
-    out_ref[FEATS + 1] = jnp.broadcast_to(
-        jnp.concatenate([cam_ref[...], jnp.zeros((1, LANES - 6), jnp.float32)], axis=1),
-        (blocks, LANES),
-    )
+        extra[b : b + 1, :] = visible_ref[:, b * LANES : (b + 1) * LANES].astype(jnp.float32)
+    extra[blocks : blocks + 8, :] = jnp.broadcast_to(
+        jnp.concatenate([cam_ref[...], jnp.zeros((1, LANES - 6), jnp.float32)], axis=1), (8, LANES)
+    )
+    project_kernel(params_ref, cam_ref, plan_ref, outgoing, staged, table, last, plan_order)
+    pl.semaphore_wait(barrier, cells + views - 2)
+
+    first = send_all(
+        "cells", cell, cells, lambda p: outgoing.at[p], lambda p: incoming.at[p], send_one, recv_one
+    )
+    keep = pltpu.make_async_copy(outgoing.at[cell], incoming.at[cell], local_sem.at[0])
+    keep.start()
+    fourth = send_all(
+        "views", view, views,
+        lambda p: extra, lambda p: shared_ref.at[p, grads : grads + blocks + 8, :],
+        send_four, recv_four,
+    )
+    keep_extra = pltpu.make_async_copy(
+        extra, shared_ref.at[view, grads : grads + blocks + 8, :], local_sem.at[1]
+    )
+    keep_extra.start()
+    keep.wait()
+    for copy in first:
+        copy.wait()
+    render_kernel(
+        cells, incoming, lists_ref, target_ref, back,
+        order, picks, wanted, before, after, alpha_s, trans_s, flow_s, parts_s, pair_s, lhs, hot,
+    )
+    second = send_all(
+        "cells", cell, cells, lambda p: back.at[p], lambda p: returned.at[p], send_two, recv_two
+    )
+    keep = pltpu.make_async_copy(back.at[cell], returned.at[cell], local_sem.at[2])
+    keep.start()
+    keep.wait()
+    for copy in second:
+        copy.wait()
+    owner_rows(returned, plan_ref, mine, own_lhs, own_hot, spread)
+    third = send_all(
+        "views", view, views,
+        lambda p: mine, lambda p: shared_ref.at[p, 0:grads, :],
+        send_three, recv_three,
+    )
+    keep = pltpu.make_async_copy(mine, shared_ref.at[view, 0:grads, :], local_sem.at[3])
+    keep.start()
+    keep.wait()
+    keep_extra.wait()
+    for copy in fourth:
+        copy.wait()
+    for copy in third:
+        copy.wait()
 
 
 def update_kernel(params_ref, first_ref, second_ref, shared_ref, new_ref, new_first_ref, new_second_ref, staged, grads):
@@ -696,11 +738,11 @@
         part, view = lax.div(step, views), lax.rem(step, views)
         base = part * (8 * PAD_ROWS)
         start = pl.multiple_of(part * 8, 8)
-        cam = shared_ref[view, FEATS + 1, 0:1, :]
+        cam = shared_ref[view, (FEATS + 1) * blocks : (FEATS + 1) * blocks + 1, :]
         turn, centre = camera_terms(cam)
         rows = tuple(staged[pl.ds(base + r, 8, stride=PAD_ROWS), :] for r in range(count))
         feats, pull = jax.vjp(lambda *items: project_rows(items, turn, centre), *rows)
-        got = [shared_ref[view, f, pl.ds(start, 8), :] for f in range(FEATS)]
+        got = [shared_ref[view, pl.ds(f * blocks + start, 8), :] for f in range(FEATS)]
         slopes = (
             feats[2] * got[1] + feats[3] * got[2],
             feats[3] * got[1] + feats[4] * got[2],
@@ -734,9 +776,9 @@
         span = slice(b * LANES, (b + 1) * LANES)
         gradient = grads[b * PAD_ROWS : b * PAD_ROWS + count, :]
         params, first, second = params_ref[:, span], first_ref[:, span], second_ref[:, span]
-        counts = shared_ref[0, FEATS, b : b + 1, :]
+        counts = shared_ref[0, FEATS * blocks + b : FEATS * blocks + b + 1, :]
         for view in range(1, views):
-            counts = counts + shared_ref[view, FEATS, b : b + 1, :]
+            counts = counts + shared_ref[view, FEATS * blocks + b : FEATS * blocks + b + 1, :]
         seen = jnp.broadcast_to(counts, params.shape) > 0.0
         first_new = 0.9 * first + 0.1 * gradient
         second_new = 0.999 * second + 0.001 * gradient * gradient
@@ -747,7 +789,7 @@
 
 
 def fused_shards(params, first_moment, second_moment, cameras, visible, send_plan, tile_lists, target):
-    cells = lax.axis_size("cells")
+    cells, views = lax.axis_size("cells"), lax.axis_size("views")
     count, block = params.shape
     blocks = block // LANES
     plan = send_plan[0, 0]
@@ -756,22 +798,20 @@
     halves = plan.shape[1] // LANES
     slots = cells * halves
     f32, bf16 = jnp.float32, jnp.bfloat16
-    packet = jax.ShapeDtypeStruct((cells, FEATS * halves, LANES), f32)
-    outgoing = pl.pallas_call(
-        project_kernel,
-        out_shape=packet,
+    packet = pltpu.VMEM((cells, FEATS * halves, LANES), f32)
+    dma = pltpu.SemaphoreType.DMA
+    shared = pl.pallas_call(
+        main_kernel,
+        out_shape=jax.ShapeDtypeStruct((views, (FEATS + 1) * blocks + 8, LANES), f32),
+        out_specs=pl.BlockSpec(memory_space=pltpu.VMEM),
         scratch_shapes=[
             pltpu.VMEM((blocks * PAD_ROWS, LANES), f32),
             pltpu.VMEM((blocks * 8, LANES), f32),
             pltpu.VMEM((blocks, LANES), f32),
             pltpu.VMEM((slots, LANES), jnp.int32),
-        ],
-    )(params, cameras, plan)
-    incoming = exchange(outgoing, "cells", True, 0)
-    back = pl.pallas_call(
-        functools.partial(render_kernel, cells),
-        out_shape=packet,
-        scratch_shapes=[
+            packet, packet, packet, packet,
+            pltpu.VMEM((FEATS * blocks, LANES), f32),
+            pltpu.VMEM((blocks + 8, LANES), f32),
             pltpu.VMEM((tiles * entries // LANES, LANES), jnp.int32),
             pltpu.VMEM((tiles, 16, entries), f32),
             pltpu.VMEM((tiles * 256, 8), f32),
@@ -784,19 +824,15 @@
             pltpu.VMEM((16, entries), f32),
             pltpu.VMEM((slots * 48, tiles * entries), bf16),
             pltpu.VMEM((LANES, tiles * entries), bf16),
-        ],
-    )(incoming, lists, target[0])
-    returned = exchange(back, "cells", True, 1)
-    mine = pl.pallas_call(
-        owner_kernel,
-        out_shape=jax.ShapeDtypeStruct((FEATS + 2, blocks, LANES), f32),
-        scratch_shapes=[
             pltpu.VMEM((blocks * 48, slots * LANES), bf16),
             pltpu.VMEM((LANES, slots * LANES), bf16),
             pltpu.VMEM((blocks * 16, LANES), f32),
+            dma((cells - 1,)), dma((cells - 1,)), dma((cells - 1,)), dma((cells - 1,)),
+            dma((views - 1,)), dma((views - 1,)), dma((views - 1,)), dma((views - 1,)),
+            dma((4,)),
         ],
-    )(returned, plan, visible, cameras)
-    shared = exchange(mine, "views", False, 2)
+        compiler_params=pltpu.CompilerParams(collective_id=0, has_side_effects=True),
+    )(params, cameras, plan, visible, lists, jnp.transpose(target, (1, 0, 2)))
     like = jax.ShapeDtypeStruct(params.shape, f32)
     return tuple(
         pl.pallas_call(

time: 55.7 us -> 44.7 us (0.80)
  Pallas kernels: 53.3 us -> 43.9 us
  local copies, waits for them, and re-layouts: 1.32 us -> 0 us
    pallas_call x6 -> x1, Pallas kernels: 45.5 us -> 36.2 us  [fused_shards(): pl.pallas_call(main_kernel, out_shape=jax.ShapeDtypeStruct((views, (FEATS...]
    unnamed x1 -> x0, local copies, waits for them, and re-layouts: 1.32 us -> none
where the time goes in v1:
time: 44.7 us; the launch traced here: 44.6 us
  Pallas kernels  43.9 us (98%)
  between operations  0.64 us (1%)
    pallas_call x1, Pallas kernels, fused_shards(): pl.pallas_call(main_kernel, out_shape=jax.ShapeDtypeStruct((views, (FEATS...  36.2 us
    pallas_call x1, Pallas kernels, fused_shards(): pl.pallas_call(update_kernel, out_shape=(like, like, like), scratch_shape...  7.76 us

profile of v1, /device:TPU:1, one launch (start us, length us, event | category | flops | bytes accessed | tf_op | source)
XLA Modules:
  0.0 44.6 jit_solution(2082945978009651703)
XLA Ops:
  0.6 36.2 %shard_map.103.shared_ref = f32[4,168,128]{2,1,0:T(8,128)} custom-call(f32[59,2048]{1,0:T(8,128)} %params_ref.3, f32[1,6]{1,0:T(1,128)} %cam_ref.1, s32[8,256]{1,0:T(8,128)} %bitcast.4, s32[1,2048]{1,0:T(1,128)} %visible_ref.1, s32[4,512]{1,0:T(4,128)} %bitcast.5, f32[3,1,1024]{2,1,0:T(1,128)} %bitcast.3), custom_call_target="tpu_custom_call" | custom-call | tf_op jit(solution)/shard_map/pallas_call | solution.py:803
  36.8 7.8 %shard_map.104 = (f32[59,2048]{1,0:T(8,128)}, f32[59,2048]{1,0:T(8,128)}, f32[59,2048]{1,0:T(8,128)}) custom-call(f32[59,2048]{1,0:T(8,128)} %params_ref.3, f32[59,2048]{1,0:T(8,128)} %first_ref.1, f32[59,2048]{1,0:T(8,128)} %second_ref.1, f32[4,168,128]{2,1,0:T(8,128)} %shard_map.103.shared_ref), custom_call_target="tpu_custom_call" | custom-call | tf_op jit(solution)/shard_map/pallas_call | solution.py:838

commit v2 on v1

--- a/solution.py
+++ b/solution.py
@@ -382,11 +382,20 @@
     centre = [cam[:, 3 + i : 4 + i] for i in range(3)]
     return turn, centre
 
-
-def stage_rows(params_ref, staged):
+def fill_dense(params_ref, dense):
     count, block = params_ref.shape
     for b in range(block // LANES):
-        staged[b * PAD_ROWS : b * PAD_ROWS + count, :] = params_ref[:, b * LANES : (b + 1) * LANES]
+        part, line = divmod(b, 8)
+        for r in range(0, count, 8):
+            size = min(8, count - r)
+            where = pl.ds((part * PAD_ROWS + r) * 8 + line, size, stride=8)
+            dense[where, :] = params_ref[r : r + size, b * LANES : (b + 1) * LANES]
+
+
+def dense_rows(dense, part, count):
+    return [
+        dense[pl.ds(pl.multiple_of((part * PAD_ROWS + r) * 8, 8), 8), :] for r in range(count)
+    ]
 
 
 def lane_pick(source, lanes):
@@ -409,41 +418,40 @@
     return first, second, rest - second
 
 
-def scatter_fill(g, index, lhs, hot, start):
-    width = g.shape[1]
-    parts = jnp.concatenate(split_three(g), axis=0)
-    high, low = index >> 7, index & (LANES - 1)
-    blocks = lhs.shape[0] // parts.shape[0]
-    size = parts.shape[0]
-    for b in range(blocks):
-        lhs[b * size : (b + 1) * size, pl.ds(start, width)] = jnp.where(
-            high == b, parts, 0.0
-        ).astype(jnp.bfloat16)
-    lane_ids = lax.broadcasted_iota(jnp.int32, (LANES, width), 0)
-    hot[:, pl.ds(start, width)] = jnp.where(lane_ids == low, 1.0, 0.0).astype(jnp.bfloat16)
+def fill_hot(hot, index, start, bits):
+    row_ids = lax.broadcasted_iota(jnp.int32, (hot.shape[0], LANES), 0)
+    low = index & ((1 << bits) - 1)
+    hot[:, start : start + LANES] = jnp.where(row_ids == low, 1.0, 0.0).astype(jnp.bfloat16)
+
+
+def fill_values(lhs, main, last, index, start, bits):
+    parts = jnp.concatenate(
+        [*split_three(main), *split_three(last), jnp.zeros((5, LANES), jnp.float32)], axis=0
+    )
+    high = jnp.broadcast_to(index >> bits, parts.shape)
+    for b in range(lhs.shape[0] // 32):
+        lhs[32 * b : 32 * b + 32, pl.ds(start, LANES)] = jnp.where(high == b, parts, 0.0).astype(
+            jnp.bfloat16
+        )
 
 
 def scatter_finish(lhs, hot):
     out = lax.dot_general(
         lhs[...], hot[...], (((1,), (1,)), ((), ())), preferred_element_type=jnp.float32
     )
-    blocks = lhs.shape[0] // 48
-    return [
-        out[48 * b : 48 * b + 16] + out[48 * b + 16 : 48 * b + 32] + out[48 * b + 32 : 48 * b + 48]
-        for b in range(blocks)
-    ]
-
-
-def project_kernel(params_ref, cam_ref, plan_ref, out_ref, staged, table, last, order):
-    count, block = params_ref.shape
-    blocks = block // LANES
+    pieces = []
+    for b in range(lhs.shape[0] // 32):
+        rows = out[32 * b : 32 * b + 32]
+        pieces.append(
+            (rows[0:8] + rows[8:16] + rows[16:24], rows[24:25] + rows[25:26] + rows[26:27])
+        )
+    return pieces
+
+
+def send_features(feat_parts, plan_ref, out_ref, table, last, order):
     halves = plan_ref.shape[1] // LANES
-    stage_rows(params_ref, staged)
-    turn, centre = camera_terms(cam_ref[...])
-    for part in range(blocks // 8):
-        base = part * 8 * PAD_ROWS
-        rows = [staged[pl.ds(base + r, 8, stride=PAD_ROWS), :] for r in range(count)]
-        feats = project_rows(rows, turn, centre)
+    blocks = last.shape[0]
+    for part, feats in enumerate(feat_parts):
         for f in range(8):
             table[pl.ds(part * 64 + f, 8, stride=8), :] = feats[f]
         last[part * 8 : part * 8 + 8, :] = feats[8]
@@ -465,186 +473,262 @@
             out_ref[8 // halves * p + i, 8 * halves :, :] = picked[i * halves : (i + 1) * halves]
 
 
-def render_kernel(
-    cells, recv_ref, lists_ref, target_ref, out_ref,
-    order, picks, wanted, before, after, alpha_s, trans_s, flow_s, parts_s, pair_s, lhs, hot,
+def pixel_terms():
+    lane = lax.broadcasted_iota(jnp.int32, (8, LANES), 1)
+    inner = lane & 31
+    tile = lane >> 5
+    x = (inner & 15).astype(jnp.float32) - 7.5
+    step = (inner >> 4).astype(jnp.float32) - 0.5
+    return tile, x, step
+
+
+def render_setup(lists_ref, target_ref, order, wanted, basis, slopes, hot, bits):
+    tiles, entries = lists_ref.shape
+    quarters = entries // LANES
+    for q in range(quarters):
+        order[q * tiles : (q + 1) * tiles, :] = lists_ref[:, q * LANES : (q + 1) * LANES]
+    sub = lax.broadcasted_iota(jnp.int32, (8, LANES), 0)
+    lane = lax.broadcasted_iota(jnp.int32, (8, LANES), 1)
+    tile, x, step = pixel_terms()
+    shifted = 32 * (sub & 3) + (lane & 31)
+    for k in range(3):
+        total = jnp.zeros((8, LANES), jnp.float32)
+        for r in range(8):
+            row = jnp.broadcast_to(target_ref[k, :, r * LANES : (r + 1) * LANES], (8, LANES))
+            here = (tile == r // 2) & ((sub >> 2) == r % 2)
+            total = jnp.where(here, lane_pick(row, shifted), total)
+        wanted[8 * k : 8 * k + 8, :] = total
+    for g in range(LANES // 8):
+        row = sub + 8 * g
+        coef = (row * 43) >> 9
+        mine = tile == (row & 3)
+
+        def column(j, *terms):
+            total = jnp.zeros((8, LANES), jnp.float32)
+            for c, value in terms:
+                total = jnp.where(coef == c, value, total)
+            total = jnp.where(mine, total, 0.0)
+            basis[8 * g : 8 * g + 8, j * LANES : (j + 1) * LANES] = total
+
+        column(0, (0, x * x), (1, x * step), (2, step * step), (3, x), (4, step), (5, 1.0))
+        column(1, (1, x), (2, 2.0 * step), (4, 1.0))
+        column(2, (2, 1.0))
+        for k in range(3):
+            column(3 + k, (6 + k, 1.0))
+    mine = tile == (sub & 3)
+    blank = jnp.zeros((LANES, LANES), jnp.bfloat16)
+    for s in range(8):
+        y = step + (2.0 * s - 7.0)
+        rows = [jnp.ones_like(x), x, y, x * x, x * y, y * y]
+        rows = jnp.concatenate(
+            [jnp.where(mine, item, 0.0) for item in rows] + [jnp.zeros((80, LANES), jnp.float32)],
+            axis=0,
+        ).astype(jnp.bfloat16)
+        for part in range(2):
+            start = (part * 8 + s) * 2 * LANES
+            slopes[:, start : start + LANES] = rows
+            slopes[:, start + LANES : start + 2 * LANES] = blank
+    for o in range(tiles * quarters):
+        fill_hot(hot, order[o : o + 1, :], o * LANES, bits)
+
+
+def render_rest(
+    cells, recv_ref, order, wanted, back_ref,
+    coefs, tables, basis, alpha_s, weight_s, slope_s, joint, slopes, moved, pairs, lhs, hot, bits,
 ):
-    tiles, entries = lists_ref.shape
     owners, packed, _ = recv_ref.shape
     halves = packed // FEATS
     blocks = owners * halves
-    quarters = entries // LANES
+    tiles = 4
+    quarters = order.shape[0] // tiles
+    entries = quarters * LANES
     me = lax.axis_index("cells")
     rows_pix = tiles * cells // TILE_COLS * 16
     half_width = TILE_COLS * 8.0
-    wanted[...] = jnp.transpose(
-        jnp.concatenate(
-            [target_ref[k] for k in range(3)] + [jnp.zeros((5, target_ref.shape[2]), jnp.float32)],
-            axis=0,
+    inv_width = 1.0 / half_width
+    log_two = 1.4426950408889634
+    sub = lax.broadcasted_iota(jnp.int32, (8, LANES), 0)
+    local = sub & 3
+    tile_col = 4 * lax.rem(me, TILE_COLS // 4) + local
+    tile_row = lax.div(me, TILE_COLS // 4)
+    centre_col = (16 * tile_col + 8).astype(jnp.float32) - half_width
+    centre_row = (jnp.full((8, LANES), 16 * tile_row + 8, jnp.int32)).astype(
+        jnp.float32
+    ) - rows_pix * 0.5
+
+    def load(f):
+        def get(b):
+            s, h = divmod(b, halves)
+            r = 8 * h + f if f < 8 else 8 * halves + h
+            return jnp.broadcast_to(recv_ref[s, r : r + 1, :], (8, LANES))
+
+        return get
+
+    for p in range(quarters // 2):
+        index = order[8 * p : 8 * p + 8, :]
+        feats = [gather_eight(load(f), blocks, index) for f in range(FEATS)]
+        off_col = feats[0] * half_width - centre_col
+        off_row = feats[1] * half_width - centre_row
+        moved[16 * p : 16 * p + 8, :] = off_col
+        moved[16 * p + 8 : 16 * p + 16, :] = off_row
+        square = feats[2] * (-0.5 * log_two * inv_width * inv_width)
+        cross = feats[3] * (-log_two * inv_width * inv_width)
+        bend = feats[4] * (-0.5 * log_two * inv_width * inv_width)
+        faint = jnp.maximum(jnp.log(feats[5]) * log_two, -1e30)
+        along = square * off_col + cross * off_row
+        level = along * off_col + bend * off_row * off_row + jnp.where(index >= 0, faint, -1e30)
+        terms = [
+            square,
+            cross,
+            bend,
+            -(along + square * off_col),
+            -(2.0 * bend * off_row + cross * off_col),
+            level,
+            feats[6],
+            feats[7],
+            feats[8],
+        ]
+        for c, term in enumerate(terms):
+            for i, piece in enumerate(split_three(term)):
+                row = (3 * c + i) * tiles
+                for q in range(2):
+                    start = (2 * p + q) * LANES
+                    coefs[start + row : start + row + tiles, :] = piece[4 * q : 4 * q + 4]
+    for q in range(quarters):
+        coefs[q * LANES + 108 : (q + 1) * LANES, :] = jnp.zeros((LANES - 108, LANES), jnp.float32)
+    weights = basis[...].astype(jnp.bfloat16)
+    for q in range(quarters):
+        span = slice(q * LANES, (q + 1) * LANES)
+        turned = jnp.transpose(coefs[span, :]).astype(jnp.bfloat16)
+        result = jnp.dot(turned, weights, preferred_element_type=jnp.float32)
+        for j in range(6):
+            tables[j, span, :] = result[:, j * LANES : (j + 1) * LANES]
+
+    height = (2 * sub - 7).astype(jnp.float32)
+
+    def table(l, j):
+        return jnp.broadcast_to(tables[j, pl.ds(l, 1), :], (8, LANES))
+
+    def forward(l, carry):
+        trans, red, green, blue = carry
+        power = table(l, 0) + height * (table(l, 1) + height * table(l, 2))
+        alpha = jnp.exp2(power)
+        weight = alpha * trans
+        where = pl.ds(pl.multiple_of(l * 8, 8), 8)
+        alpha_s[where, :] = alpha
+        weight_s[where, :] = weight
+        return (
+            trans * (1.0 - alpha),
+            red + weight * table(l, 3),
+            green + weight * table(l, 4),
+            blue + weight * table(l, 5),
         )
-    )
-    row_ids = lax.broadcasted_iota(jnp.int32, (entries, entries), 0)
-    col_ids = lax.broadcasted_iota(jnp.int32, (entries, entries), 1)
-    before[...] = jnp.where(row_ids < col_ids, 1.0, 0.0).astype(jnp.bfloat16)
-    after[...] = jnp.where(row_ids > col_ids, 1.0, 0.0).astype(jnp.bfloat16)
-
-    def load_main(b):
-        s, h = divmod(b, halves)
-        return recv_ref[s, 8 * h : 8 * h + 8, :]
-
-    def load_last(b):
-        s, h = divmod(b, halves)
-        return jnp.broadcast_to(recv_ref[s, 8 * halves + h : 8 * halves + h + 1, :], (8, LANES))
-
-    slots = tiles * quarters
-    for o in range(slots):
-        t, q = divmod(o, quarters)
-        row = lists_ref[t : t + 1, q * LANES : (q + 1) * LANES]
-        order[o : o + 1, :] = row
-        picks[t, 0:8, q * LANES : (q + 1) * LANES] = gather_eight(
-            load_main, blocks, jnp.broadcast_to(row, (8, LANES))
+
+    zero = jnp.zeros((8, LANES), jnp.float32)
+    _, red, green, blue = lax.fori_loop(
+        0, entries, forward, (jnp.ones((8, LANES), jnp.float32), zero, zero, zero), unroll=16
+    )
+    errors = [2.0 * (item - wanted[8 * k : 8 * k + 8, :]) for k, item in enumerate((red, green, blue))]
+    wanted[0:8, :], wanted[8:16, :], wanted[16:24, :] = errors
+    tile, _, _ = pixel_terms()
+    mine = tile == local
+    for s in range(8):
+        tops, lows = [], []
+        for k in range(3):
+            row = jnp.broadcast_to(wanted[8 * k + s : 8 * k + s + 1, :], (8, LANES))
+            row = jnp.where(mine, row, 0.0)
+            top = row.astype(jnp.bfloat16).astype(jnp.float32)
+            tops.append(top)
+            lows.append(row - top)
+        tops = jnp.concatenate(tops + lows, axis=0).astype(jnp.bfloat16)
+        start = s * 2 * LANES + LANES
+        slopes[48:96, start : start + LANES] = tops
+        start = start + 16 * LANES
+        slopes[48:72, start : start + LANES] = tops[0:24]
+
+    def backward(i, behind):
+        l = entries - 1 - i
+        where = pl.ds(pl.multiple_of(l * 8, 8), 8)
+        slope = errors[0] * table(l, 3) + errors[1] * table(l, 4) + errors[2] * table(l, 5)
+        above = slope - behind
+        slope_s[where, :] = weight_s[where, :] * above
+        return behind + alpha_s[where, :] * above
+
+    lax.fori_loop(0, entries, backward, zero, unroll=16)
+
+    def relay(c, carry):
+        rows = pl.ds(pl.multiple_of(c * 16, 16), 16)
+        for s in range(8):
+            for part, source in enumerate((slope_s, weight_s)):
+                item = source[pl.ds(c * 128 + s, 16, stride=8), :]
+                top = item.astype(jnp.bfloat16)
+                start = s * 2 * LANES + part * LANES
+                joint[rows, start : start + LANES] = top
+                start = start + 16 * LANES
+                joint[rows, start : start + LANES] = (item - top.astype(jnp.float32)).astype(
+                    jnp.bfloat16
+                )
+        return carry
+
+    lax.fori_loop(0, entries // 16, relay, 0, unroll=2)
+    sums = lax.dot_general(
+        joint[...], slopes[...], (((1,), (1,)), ((), ())), preferred_element_type=jnp.float32
+    )
+    turned = [jnp.transpose(sums[q * LANES : (q + 1) * LANES]) for q in range(quarters)]
+    for p in range(quarters // 2):
+        off_col = moved[16 * p : 16 * p + 8, :]
+        off_row = moved[16 * p + 8 : 16 * p + 16, :]
+
+        def quantity(j):
+            span = slice(8 * j, 8 * j + 8)
+            return jnp.where(sub < 4, turned[2 * p][span], turned[2 * p + 1][span])
+
+        plain, across, down = quantity(0), quantity(1), quantity(2)
+        near_col = across - off_col * plain
+        near_row = down - off_row * plain
+        rows = [
+            plain,
+            near_col * inv_width,
+            near_row * inv_width,
+            (quantity(3) - off_col * (across + near_col)) * (inv_width * inv_width),
+            (quantity(4) - off_col * down - off_row * near_col) * (inv_width * inv_width),
+            (quantity(5) - off_row * (down + near_row)) * (inv_width * inv_width),
+            *[quantity(6 + k) + quantity(9 + k) for k in range(3)],
+        ]
+        for f, item in enumerate(rows):
+            pairs[pl.ds(p * 128 + f, 8, stride=16), :] = item
+    for o in range(tiles * quarters):
+        fill_values(
+            lhs,
+            pairs[o * 16 : o * 16 + 8, :],
+            pairs[o * 16 + 8 : o * 16 + 9, :],
+            order[o : o + 1, :],
+            o * LANES,
+            bits,
         )
-    for p in range(slots // 8):
-        picked = gather_eight(load_last, blocks, order[8 * p : 8 * p + 8, :])
-        for i in range(8):
-            t, q = divmod(8 * p + i, quarters)
-            picks[t, 8:9, q * LANES : (q + 1) * LANES] = picked[i : i + 1]
-
-    def one_tile(t, carry):
-        def feature(f):
-            return picks[t, f : f + 1, :]
-
-        listed = lists_ref[pl.ds(t, 1), :]
-        opacity = jnp.where(listed >= 0, feature(5), 0.0)
-        tile_col = 4 * lax.rem(me, TILE_COLS // 4) + lax.rem(t, 4)
-        tile_row = tiles // 4 * lax.div(me, TILE_COLS // 4) + lax.div(t, 4)
-        across = (lax.broadcasted_iota(jnp.int32, (16, entries), 0) + tile_col * 16).astype(jnp.float32)
-        delta_col = (across + 0.5 - half_width) * (1.0 / half_width) - feature(0)
-        square_term = -0.5 * feature(2) * delta_col * delta_col
-        cross_term = -feature(3) * delta_col
-        row_scale = -0.5 * feature(4)
-
-        def delta_row_at(r):
-            down = (jnp.full((1, entries), tile_row * 16 + r, jnp.int32)).astype(jnp.float32)
-            return (down + 0.5 - rows_pix * 0.5) * (1.0 / half_width) - feature(1)
-
-        def put_parts(r, x):
-            first = x.astype(jnp.bfloat16)
-            parts_s[pl.ds(r * 16, 16), :] = first
-            parts_s[pl.ds(256 + r * 16, 16), :] = (x - first.astype(jnp.float32)).astype(jnp.bfloat16)
-
-        def forward(r, carry):
-            delta_row = delta_row_at(r)
-            power = square_term + cross_term * delta_row + row_scale * delta_row * delta_row
-            alpha = opacity * jnp.exp(power)
-            alpha_s[pl.ds(r * 16, 16), :] = alpha
-            put_parts(r, jnp.log(1.0 - alpha))
-            return carry
-
-        lax.fori_loop(0, 16, forward, 0, unroll=4)
-        sums = jnp.dot(parts_s[...], before[...], preferred_element_type=jnp.float32)
-        trans_s[...] = jnp.exp(sums[0:256] + sums[256:512])
-
-        def errors_of(r, carry):
-            weight = alpha_s[pl.ds(r * 16, 16), :] * trans_s[pl.ds(r * 16, 16), :]
-            where = pl.ds(t * 256 + r * 16, 16)
-            values = [jnp.sum(weight * feature(6 + k), axis=1, keepdims=True) for k in range(3)]
-            lane = lax.broadcasted_iota(jnp.int32, (16, 8), 1)
-            image = jnp.where(lane == 0, values[0], jnp.where(lane == 1, values[1], values[2]))
-            wanted[where, :] = 2.0 * (image - wanted[where, :])
-            return carry
-
-        lax.fori_loop(0, 16, errors_of, 0, unroll=8)
-
-        def colors_of(r, carry):
-            weight = alpha_s[pl.ds(r * 16, 16), :] * trans_s[pl.ds(r * 16, 16), :]
-            errors = wanted[pl.ds(t * 256 + r * 16, 16), :]
-            slope = 0.0
-            sums = []
-            for k in range(3):
-                error = errors[:, k : k + 1]
-                slope = slope + error * feature(6 + k)
-                sums.append(carry[k] + error * weight)
-            flow = weight * slope
-            flow_s[pl.ds(r * 16, 16), :] = flow
-            put_parts(r, flow)
-            return tuple(sums)
-
-        empty = jnp.zeros((16, entries), jnp.float32)
-        color_sums = lax.fori_loop(0, 16, colors_of, (empty, empty, empty), unroll=4)
-        sums = jnp.dot(parts_s[...], after[...], preferred_element_type=jnp.float32)
-        trans_s[...] = sums[0:256] + sums[256:512]
-
-        def backward(r, carry):
-            delta_row = delta_row_at(r)
-            alpha = alpha_s[pl.ds(r * 16, 16), :]
-            slope = flow_s[pl.ds(r * 16, 16), :] - alpha / (1.0 - alpha) * trans_s[pl.ds(r * 16, 16), :]
-            return (
-                carry[0] + slope,
-                carry[1] + slope * delta_row,
-                carry[2] + slope * (delta_row * delta_row),
-            )
-
-        plain, tilted, bent = lax.fori_loop(0, 16, backward, (empty, empty, empty), unroll=4)
-
-        def fold(x):
-            return jnp.sum(x, axis=0, keepdims=True)
-
-        moved = plain * delta_col
-        pair_s[...] = jnp.concatenate(
-            [
-                fold(plain),
-                fold(moved),
-                fold(tilted),
-                fold(moved * delta_col),
-                fold(tilted * delta_col),
-                fold(bent),
-                fold(color_sums[0]),
-                fold(color_sums[1]),
-                fold(color_sums[2]),
-                jnp.zeros((7, entries), jnp.float32),
-            ],
-            axis=0,
-        )
-        scatter_fill(pair_s[...], listed, lhs, hot, pl.multiple_of(t * entries, entries))
-        return carry
-
-    lax.fori_loop(0, tiles, one_tile, 0)
-    for b, piece in enumerate(scatter_finish(lhs, hot)):
-        s, h = divmod(b, halves)
-        out_ref[s, 8 * h : 8 * h + 8, :] = piece[0:8]
-        out_ref[s, 8 * halves + h : 8 * halves + h + 1, :] = piece[8:9]
-
-
-def owner_rows(back_ref, plan_ref, out_ref, lhs, hot, spread):
-    devices, packed, _ = back_ref.shape
-    halves = packed // FEATS
-    for d in range(devices):
-        main = jnp.concatenate([back_ref[d, 8 * h : 8 * h + 8, :] for h in range(halves)], axis=1)
-        last = jnp.concatenate(
-            [back_ref[d, 8 * halves + h : 8 * halves + h + 1, :] for h in range(halves)], axis=1
-        )
-        g = jnp.concatenate([main, last, jnp.zeros((7, halves * LANES), jnp.float32)], axis=0)
-        scatter_fill(g, plan_ref[d : d + 1, :], lhs, hot, d * halves * LANES)
-    pieces = scatter_finish(lhs, hot)
-    blocks = len(pieces)
-    for b, piece in enumerate(pieces):
-        spread[16 * b : 16 * b + 16, :] = piece
-    for f in range(FEATS):
-        out_ref[f * blocks : (f + 1) * blocks, :] = spread[pl.ds(f, blocks, stride=16), :]
+    for s, (main, last) in enumerate(scatter_finish(lhs, hot)):
+        for h in range(halves):
+            span = slice(h * LANES, (h + 1) * LANES)
+            back_ref[s, 8 * h : 8 * h + 8, :] = main[:, span]
+            back_ref[s, 8 * halves + h : 8 * halves + h + 1, :] = last[:, span]
 
 
 def main_kernel(
-    params_ref, cam_ref, plan_ref, visible_ref, lists_ref, target_ref, shared_ref,
-    staged, table, last, plan_order, outgoing, incoming, back, returned, mine, extra,
-    order, picks, wanted, before, after, alpha_s, trans_s, flow_s, parts_s, pair_s, lhs, hot,
-    own_lhs, own_hot, spread,
+    params_ref, cam_ref, plan_ref, visible_ref, lists_ref, target_ref, out_ref,
+    held, dense, table, last, plan_order, outgoing, incoming, back, returned, mine, extra, extras, shared,
+    order, wanted, basis, coefs, tables, alpha_s, weight_s, slope_s, joint, slopes, moved, pairs,
+    lhs, hot, own_lhs, own_hot,
     send_one, recv_one, send_two, recv_two, send_three, recv_three, send_four, recv_four, local_sem,
 ):
     cells, views = lax.axis_size("cells"), lax.axis_size("views")
     cell, view = lax.axis_index("cells"), lax.axis_index("views")
-    blocks = params_ref.shape[1] // LANES
-    grads = FEATS * blocks
+    count, block = params_ref.shape
+    blocks = block // LANES
+    capacity = plan_ref.shape[1]
+    halves = capacity // LANES
+    bits = capacity.bit_length() - 1
+    fetch = pltpu.make_async_copy(params_ref, held, local_sem.at[0])
+    fetch.start()
     barrier = pltpu.get_barrier_semaphore()
 
     def greet(axis, me, size):
@@ -676,116 +760,144 @@
     greet("views", view, views)
     for b in range(blocks):
         extra[b : b + 1, :] = visible_ref[:, b * LANES : (b + 1) * LANES].astype(jnp.float32)
-    extra[blocks : blocks + 8, :] = jnp.broadcast_to(
-        jnp.concatenate([cam_ref[...], jnp.zeros((1, LANES - 6), jnp.float32)], axis=1), (8, LANES)
-    )
-    project_kernel(params_ref, cam_ref, plan_ref, outgoing, staged, table, last, plan_order)
+    turn, centre = camera_terms(cam_ref[...])
+    known = [*turn[0], *turn[1], *turn[2], *centre]
+    lane = lax.broadcasted_iota(jnp.int32, (8, LANES), 1)
+    line = jnp.zeros((8, LANES), jnp.float32)
+    for i, item in enumerate(known):
+        line = jnp.where(lane == i, jnp.broadcast_to(item, (8, LANES)), line)
+    extra[blocks : blocks + 8, :] = line
+    fetch.wait()
+    fill_dense(held, dense)
+    feat_parts = [
+        project_rows(dense_rows(dense, part, count), turn, centre) for part in range(blocks // 8)
+    ]
+    send_features(feat_parts, plan_ref, outgoing, table, last, plan_order)
     pl.semaphore_wait(barrier, cells + views - 2)
 
     first = send_all(
         "cells", cell, cells, lambda p: outgoing.at[p], lambda p: incoming.at[p], send_one, recv_one
     )
-    keep = pltpu.make_async_copy(outgoing.at[cell], incoming.at[cell], local_sem.at[0])
-    keep.start()
     fourth = send_all(
-        "views", view, views,
-        lambda p: extra, lambda p: shared_ref.at[p, grads : grads + blocks + 8, :],
-        send_four, recv_four,
-    )
-    keep_extra = pltpu.make_async_copy(
-        extra, shared_ref.at[view, grads : grads + blocks + 8, :], local_sem.at[1]
-    )
-    keep_extra.start()
-    keep.wait()
+        "views", view, views, lambda p: extra, lambda p: extras.at[p], send_four, recv_four
+    )
+    incoming[cell] = outgoing[cell]
+    extras[view] = extra[...]
+    render_setup(lists_ref, target_ref, order, wanted, basis, slopes, hot, bits)
     for copy in first:
         copy.wait()
-    render_kernel(
-        cells, incoming, lists_ref, target_ref, back,
-        order, picks, wanted, before, after, alpha_s, trans_s, flow_s, parts_s, pair_s, lhs, hot,
+    render_rest(
+        cells, incoming, order, wanted, back,
+        coefs, tables, basis, alpha_s, weight_s, slope_s, joint, slopes, moved, pairs, lhs, hot, bits,
     )
     second = send_all(
         "cells", cell, cells, lambda p: back.at[p], lambda p: returned.at[p], send_two, recv_two
     )
-    keep = pltpu.make_async_copy(back.at[cell], returned.at[cell], local_sem.at[2])
-    keep.start()
-    keep.wait()
+    returned[cell] = back[cell]
+    wide = own_hot.shape[0].bit_length() - 1
+    for o in range(cells * halves):
+        d, h = divmod(o, halves)
+        fill_hot(own_hot, plan_ref[d : d + 1, h * LANES : (h + 1) * LANES], o * LANES, wide)
     for copy in second:
         copy.wait()
-    owner_rows(returned, plan_ref, mine, own_lhs, own_hot, spread)
+    for o in range(cells * halves):
+        d, h = divmod(o, halves)
+        fill_values(
+            own_lhs,
+            returned[d, 8 * h : 8 * h + 8, :],
+            returned[d, 8 * halves + h : 8 * halves + h + 1, :],
+            plan_ref[d : d + 1, h * LANES : (h + 1) * LANES],
+            o * LANES,
+            wide,
+        )
+    for g, (main, tip) in enumerate(scatter_finish(own_lhs, own_hot)):
+        for i in range(2):
+            span = slice(i * LANES, (i + 1) * LANES)
+            for f in range(8):
+                mine[f * blocks + 2 * g + i : f * blocks + 2 * g + i + 1, :] = main[f : f + 1, span]
+            mine[8 * blocks + 2 * g + i : 8 * blocks + 2 * g + i + 1, :] = tip[:, span]
     third = send_all(
-        "views", view, views,
-        lambda p: mine, lambda p: shared_ref.at[p, 0:grads, :],
-        send_three, recv_three,
-    )
-    keep = pltpu.make_async_copy(mine, shared_ref.at[view, 0:grads, :], local_sem.at[3])
-    keep.start()
-    keep.wait()
-    keep_extra.wait()
+        "views", view, views, lambda p: mine, lambda p: shared.at[p], send_three, recv_three
+    )
     for copy in fourth:
         copy.wait()
-    for copy in third:
-        copy.wait()
-
-
-def update_kernel(params_ref, first_ref, second_ref, shared_ref, new_ref, new_first_ref, new_second_ref, staged, grads):
+    counts = extras[0, 0:blocks, :]
+    for v in range(1, views):
+        counts = counts + extras[v, 0:blocks, :]
+    grads = blocks * PAD_ROWS
+    out_ref[grads : grads + blocks, :] = counts
+
+    def pull_view(fresh, source, lines):
+        known = [jnp.broadcast_to(lines[:, i : i + 1], (8, LANES)) for i in range(12)]
+        turn = [known[0:3], known[3:6], known[6:9]]
+        centre = known[9:12]
+
+        def one_part(part, carry):
+            rows = dense_rows(dense, part, count)
+            feats, pull = jax.vjp(lambda *items: project_rows(items, turn, centre), *rows)
+            got = [
+                source[pl.ds(pl.multiple_of(f * blocks + part * 8, 8), 8), :] for f in range(FEATS)
+            ]
+            wanted_slopes = (
+                feats[2] * got[1] + feats[3] * got[2],
+                feats[3] * got[1] + feats[4] * got[2],
+                -0.5 * got[3],
+                -got[4],
+                -0.5 * got[5],
+                got[0] / feats[5],
+                got[6],
+                got[7],
+                got[8],
+            )
+            for r, item in enumerate(pull(wanted_slopes)):
+                where = pl.ds(pl.multiple_of((part * PAD_ROWS + r) * 8, 8), 8)
+                out_ref[where, :] = item if fresh else out_ref[where, :] + item
+            return carry
+
+        lax.fori_loop(0, blocks // 8, one_part, 0)
+
+    pull_view(True, mine, extra[blocks : blocks + 1, :])
+    for k in range(1, views):
+        third[views - 1 - k].wait()
+        origin = lax.rem(view + k, views)
+        pull_view(False, shared.at[origin], extras[origin, blocks : blocks + 1, :])
+
+
+def update_kernel(params_ref, first_ref, second_ref, grads_ref, new_ref, new_first_ref, new_second_ref):
     count, block = params_ref.shape
     blocks = block // LANES
-    views = shared_ref.shape[0]
-    stage_rows(params_ref, staged)
-    grads[...] = jnp.zeros_like(grads)
-
-    def one_part(step, carry):
-        part, view = lax.div(step, views), lax.rem(step, views)
-        base = part * (8 * PAD_ROWS)
-        start = pl.multiple_of(part * 8, 8)
-        cam = shared_ref[view, (FEATS + 1) * blocks : (FEATS + 1) * blocks + 1, :]
-        turn, centre = camera_terms(cam)
-        rows = tuple(staged[pl.ds(base + r, 8, stride=PAD_ROWS), :] for r in range(count))
-        feats, pull = jax.vjp(lambda *items: project_rows(items, turn, centre), *rows)
-        got = [shared_ref[view, pl.ds(f * blocks + start, 8), :] for f in range(FEATS)]
-        slopes = (
-            feats[2] * got[1] + feats[3] * got[2],
-            feats[3] * got[1] + feats[4] * got[2],
-            -0.5 * got[3],
-            -got[4],
-            -0.5 * got[5],
-            got[0] / feats[5],
-            got[6],
-            got[7],
-            got[8],
-        )
-        for r, item in enumerate(pull(slopes)):
-            where = pl.ds(base + r, 8, stride=PAD_ROWS)
-            grads[where, :] = grads[where, :] + item
-        return carry
-
-    lax.fori_loop(0, blocks // 8 * views, one_part, 0)
-    row_ids = lax.broadcasted_iota(jnp.int32, (count, LANES), 0)
-    rates = jnp.where(
-        row_ids < 6,
-        0.01,
-        jnp.where(
-            row_ids < 10,
-            0.005,
-            jnp.where(row_ids < 11, 0.05, jnp.where(row_ids < 14, 0.0025, 0.000125)),
-        ),
-    )
+    row_ids = lax.broadcasted_iota(jnp.int32, (8, LANES), 0)
     bias_one = 1.0 - 0.9**ADAM_STEP
     bias_two = 1.0 - 0.999**ADAM_STEP
     for b in range(blocks):
         span = slice(b * LANES, (b + 1) * LANES)
-        gradient = grads[b * PAD_ROWS : b * PAD_ROWS + count, :]
-        params, first, second = params_ref[:, span], first_ref[:, span], second_ref[:, span]
-        counts = shared_ref[0, FEATS * blocks + b : FEATS * blocks + b + 1, :]
-        for view in range(1, views):
-            counts = counts + shared_ref[view, FEATS * blocks + b : FEATS * blocks + b + 1, :]
-        seen = jnp.broadcast_to(counts, params.shape) > 0.0
-        first_new = 0.9 * first + 0.1 * gradient
-        second_new = 0.999 * second + 0.001 * gradient * gradient
-        stride = rates * (first_new / bias_one) / (jnp.sqrt(second_new / bias_two) + 1e-08)
-        new_ref[:, span] = jnp.where(seen, params - stride, params)
-        new_first_ref[:, span] = jnp.where(seen, first_new, first)
-        new_second_ref[:, span] = jnp.where(seen, second_new, second)
+        part, line = divmod(b, 8)
+        counts = grads_ref[blocks * PAD_ROWS + b : blocks * PAD_ROWS + b + 1, :]
+        for r in range(0, count, 8):
+            size = min(8, count - r)
+            rows = slice(r, r + size)
+            gradient = grads_ref[pl.ds((part * PAD_ROWS + r) * 8 + line, size, stride=8), :]
+            if r >= 16:
+                rates = 0.000125
+            else:
+                ids = row_ids[0:size] + r
+                rates = jnp.where(
+                    ids < 6,
+                    0.01,
+                    jnp.where(
+                        ids < 10,
+                        0.005,
+                        jnp.where(ids < 11, 0.05, jnp.where(ids < 14, 0.0025, 0.000125)),
+                    ),
+                )
+            params, first, second = params_ref[rows, span], first_ref[rows, span], second_ref[rows, span]
+            seen = jnp.broadcast_to(counts, params.shape) > 0.0
+            first_new = 0.9 * first + 0.1 * gradient
+            second_new = 0.999 * second + 0.001 * gradient * gradient
+            stride = rates * (first_new / bias_one) / (jnp.sqrt(second_new / bias_two) + 1e-08)
+            new_ref[rows, span] = jnp.where(seen, params - stride, params)
+            new_first_ref[rows, span] = jnp.where(seen, first_new, first)
+            new_second_ref[rows, span] = jnp.where(seen, second_new, second)
 
 
 def fused_shards(params, first_moment, second_moment, cameras, visible, send_plan, tile_lists, target):
@@ -795,16 +907,20 @@
     plan = send_plan[0, 0]
     lists = tile_lists[0]
     tiles, entries = lists.shape
-    halves = plan.shape[1] // LANES
+    capacity = plan.shape[1]
+    halves = capacity // LANES
     slots = cells * halves
     f32, bf16 = jnp.float32, jnp.bfloat16
     packet = pltpu.VMEM((cells, FEATS * halves, LANES), f32)
     dma = pltpu.SemaphoreType.DMA
-    shared = pl.pallas_call(
+    vmem = pl.BlockSpec(memory_space=pltpu.VMEM)
+    grads = pl.pallas_call(
         main_kernel,
-        out_shape=jax.ShapeDtypeStruct((views, (FEATS + 1) * blocks + 8, LANES), f32),
-        out_specs=pl.BlockSpec(memory_space=pltpu.VMEM),
+        out_shape=jax.ShapeDtypeStruct((blocks * PAD_ROWS + blocks, LANES), f32),
+        in_specs=[pl.BlockSpec(memory_space=pl.ANY), vmem, vmem, vmem, vmem, vmem],
+        out_specs=vmem,
         scratch_shapes=[
+            pltpu.VMEM((count, block), f32),
             pltpu.VMEM((blocks * PAD_ROWS, LANES), f32),
             pltpu.VMEM((blocks * 8, LANES), f32),
             pltpu.VMEM((blocks, LANES), f32),
@@ -812,37 +928,35 @@
             packet, packet, packet, packet,
             pltpu.VMEM((FEATS * blocks, LANES), f32),
             pltpu.VMEM((blocks + 8, LANES), f32),
+            pltpu.VMEM((views, blocks + 8, LANES), f32),
+            pltpu.VMEM((views, FEATS * blocks, LANES), f32),
             pltpu.VMEM((tiles * entries // LANES, LANES), jnp.int32),
-            pltpu.VMEM((tiles, 16, entries), f32),
-            pltpu.VMEM((tiles * 256, 8), f32),
-            pltpu.VMEM((entries, entries), bf16),
-            pltpu.VMEM((entries, entries), bf16),
-            pltpu.VMEM((256, entries), f32),
-            pltpu.VMEM((256, entries), f32),
-            pltpu.VMEM((256, entries), f32),
-            pltpu.VMEM((512, entries), bf16),
-            pltpu.VMEM((16, entries), f32),
-            pltpu.VMEM((slots * 48, tiles * entries), bf16),
-            pltpu.VMEM((LANES, tiles * entries), bf16),
-            pltpu.VMEM((blocks * 48, slots * LANES), bf16),
-            pltpu.VMEM((LANES, slots * LANES), bf16),
-            pltpu.VMEM((blocks * 16, LANES), f32),
+            pltpu.VMEM((24, LANES), f32),
+            pltpu.VMEM((LANES, 6 * LANES), f32),
+            pltpu.VMEM((entries, LANES), f32),
+            pltpu.VMEM((6, entries, LANES), f32),
+            pltpu.VMEM((entries * 8, LANES), f32),
+            pltpu.VMEM((entries * 8, LANES), f32),
+            pltpu.VMEM((entries * 8, LANES), f32),
+            pltpu.VMEM((entries, 32 * LANES), bf16),
+            pltpu.VMEM((LANES, 32 * LANES), bf16),
+            pltpu.VMEM((entries // LANES * 8, LANES), f32),
+            pltpu.VMEM((tiles * entries // LANES * 16, LANES), f32),
+            pltpu.VMEM((cells * 32, tiles * entries), bf16),
+            pltpu.VMEM((capacity, tiles * entries), bf16),
+            pltpu.VMEM((blocks // 2 * 32, slots * LANES), bf16),
+            pltpu.VMEM((2 * LANES, slots * LANES), bf16),
             dma((cells - 1,)), dma((cells - 1,)), dma((cells - 1,)), dma((cells - 1,)),
             dma((views - 1,)), dma((views - 1,)), dma((views - 1,)), dma((views - 1,)),
-            dma((4,)),
+            dma((1,)),
         ],
         compiler_params=pltpu.CompilerParams(collective_id=0, has_side_effects=True),
     )(params, cameras, plan, visible, lists, jnp.transpose(target, (1, 0, 2)))
     like = jax.ShapeDtypeStruct(params.shape, f32)
     return tuple(
-        pl.pallas_call(
-            update_kernel,
-            out_shape=(like, like, like),
-            scratch_shapes=[
-                pltpu.VMEM((blocks * PAD_ROWS, LANES), f32),
-                pltpu.VMEM((blocks * PAD_ROWS, LANES), f32),
-            ],
-        )(params, first_moment, second_moment, shared)
+        pl.pallas_call(update_kernel, out_shape=(like, like, like))(
+            params, first_moment, second_moment, grads
+        )
     )
 
 
@@ -853,12 +967,11 @@
     fits = (
         capacity % LANES == 0
         and params.shape[1] % (8 * LANES) == 0
-        and entries % LANES == 0
+        and entries % (2 * LANES) == 0
         and 8 % max(halves, 1) == 0
         and lax.axis_size("cells") * halves % 8 == 0
-        and tiles * entries // LANES % 8 == 0
         and tiles * entries <= 4096
-        and tiles % 4 == 0
+        and tiles == 4
     )
     body = fused_shards if fits else shards
     return body(params, first_moment, second_moment, cameras, visible, send_plan, tile_lists, target)

time: 44.7 us -> 33.8 us (0.76)
  Pallas kernels: 43.9 us -> 32.9 us
    pallas_call x2, Pallas kernels: 43.9 us -> 32.9 us  [the longest x1 29.8 us: fused_shards(): pl.pallas_call(main_kernel, out_shape=jax.ShapeDtypeStruct((blocks * PAD_...]
where the time goes in v2:
time: 33.8 us; the launch traced here: 33.5 us
  Pallas kernels  32.9 us (97%)
  between operations  0.64 us (2%)
    pallas_call x1, Pallas kernels, fused_shards(): pl.pallas_call(main_kernel, out_shape=jax.ShapeDtypeStruct((blocks * PAD_...  29.8 us
    pallas_call x1, Pallas kernels, fused_shards(): pl.pallas_call(update_kernel, out_shape=(like, like, like))  3.07 us

profile of v2, /device:TPU:1, one launch (start us, length us, event | category | flops | bytes accessed | tf_op | source)
XLA Modules:
  0.0 33.5 jit_solution(7565273528737664674)
XLA Ops:
  0.6 29.8 %shard_map.103.grads_ref = f32[1040,128]{1,0:T(8,128)} custom-call(f32[59,2048]{1,0:T(8,128)} %params_ref.3, f32[1,6]{1,0:T(1,128)} %cam_ref.1, s32[8,256]{1,0:T(8,128)} %bitcast.4, s32[1,2048]{1,0:T(1,128)} %visible_ref.1, s32[4,512]{1,0:T(4,128)} %bitcast.5, f32[3,1,1024]{2,1,0:T(1,128)} %bitcast.3), custom_call_target="tpu_custom_call" | custom-call | tf_op jit(solution)/shard_map/pallas_call | solution.py:917
  30.4 3.1 %shard_map.104 = (f32[59,2048]{1,0:T(8,128)}, f32[59,2048]{1,0:T(8,128)}, f32[59,2048]{1,0:T(8,128)}) custom-call(f32[59,2048]{1,0:T(8,128)} %params_ref.3, f32[59,2048]{1,0:T(8,128)} %first_ref.1, f32[59,2048]{1,0:T(8,128)} %second_ref.1, f32[1040,128]{1,0:T(8,128)} %shard_map.103.grads_ref), custom_call_target="tpu_custom_call" | custom-call | tf_op jit(solution)/shard_map/pallas_call | solution.py:957

commit v3 on v2

--- a/solution.py
+++ b/solution.py
@@ -382,6 +382,11 @@
     centre = [cam[:, 3 + i : 4 + i] for i in range(3)]
     return turn, centre
 
+MAIN_VMEM = 40 * 2**20
+UPDATE_VMEM = 16 * 2**20
+UNROLL = 1
+
+
 def fill_dense(params_ref, dense):
     count, block = params_ref.shape
     for b in range(block // LANES):
@@ -482,7 +487,7 @@
     return tile, x, step
 
 
-def render_setup(lists_ref, target_ref, order, wanted, basis, slopes, hot, bits):
+def render_setup(lists_ref, target_ref, order, wanted, basis, plan_sums, hot, bits):
     tiles, entries = lists_ref.shape
     quarters = entries // LANES
     for q in range(quarters):
@@ -516,25 +521,21 @@
         for k in range(3):
             column(3 + k, (6 + k, 1.0))
     mine = tile == (sub & 3)
-    blank = jnp.zeros((LANES, LANES), jnp.bfloat16)
     for s in range(8):
         y = step + (2.0 * s - 7.0)
         rows = [jnp.ones_like(x), x, y, x * x, x * y, y * y]
-        rows = jnp.concatenate(
-            [jnp.where(mine, item, 0.0) for item in rows] + [jnp.zeros((80, LANES), jnp.float32)],
-            axis=0,
-        ).astype(jnp.bfloat16)
+        rows = jnp.concatenate([jnp.where(mine, item, 0.0) for item in rows], axis=0)
         for part in range(2):
-            start = (part * 8 + s) * 2 * LANES
-            slopes[:, start : start + LANES] = rows
-            slopes[:, start + LANES : start + 2 * LANES] = blank
+            start = (part * 8 + s) * LANES
+            plan_sums[:, start : start + LANES] = rows.astype(jnp.bfloat16)
     for o in range(tiles * quarters):
         fill_hot(hot, order[o : o + 1, :], o * LANES, bits)
 
 
 def render_rest(
-    cells, recv_ref, order, wanted, back_ref,
-    coefs, tables, basis, alpha_s, weight_s, slope_s, joint, slopes, moved, pairs, lhs, hot, bits,
+    cells, copies, recv_ref, order, wanted, back_ref,
+    coefs, tables, basis, alpha_s, weight_s, slope_s, joint_g, joint_w, plan_sums, error_sums,
+    moved, pairs, lhs, hot, bits,
 ):
     owners, packed, _ = recv_ref.shape
     halves = packed // FEATS
@@ -556,17 +557,26 @@
         jnp.float32
     ) - rows_pix * 0.5
 
-    def load(f):
-        def get(b):
-            s, h = divmod(b, halves)
-            r = 8 * h + f if f < 8 else 8 * halves + h
-            return jnp.broadcast_to(recv_ref[s, r : r + 1, :], (8, LANES))
-
-        return get
+    picked = [[None] * FEATS for _ in range(quarters // 2)]
+    for k in range(owners):
+        origin = lax.rem(me + owners - k, owners)
+        if k:
+            copies[k - 1].wait()
+        for p in range(quarters // 2):
+            index = jnp.maximum(order[8 * p : 8 * p + 8, :], 0)
+            lanes, block = index & (LANES - 1), index >> 7
+            for h in range(halves):
+                here = block == origin * halves + h
+                for f in range(FEATS):
+                    r = 8 * h + f if f < 8 else 8 * halves + h
+                    row = jnp.broadcast_to(recv_ref[origin, r : r + 1, :], (8, LANES))
+                    item = lane_pick(row, lanes)
+                    old = picked[p][f]
+                    picked[p][f] = item if old is None else jnp.where(here, item, old)
 
     for p in range(quarters // 2):
         index = order[8 * p : 8 * p + 8, :]
-        feats = [gather_eight(load(f), blocks, index) for f in range(FEATS)]
+        feats = picked[p]
         off_col = feats[0] * half_width - centre_col
         off_row = feats[1] * half_width - centre_row
         moved[16 * p : 16 * p + 8, :] = off_col
@@ -609,25 +619,40 @@
     def table(l, j):
         return jnp.broadcast_to(tables[j, pl.ds(l, 1), :], (8, LANES))
 
-    def forward(l, carry):
+    def relay(source, joint, c, s):
+        item = source[pl.ds(c * 128 + s, 16, stride=8), :]
+        top = item.astype(jnp.bfloat16)
+        rows = pl.ds(pl.multiple_of(c * 16, 16), 16)
+        joint[rows, s * LANES : (s + 1) * LANES] = top
+        joint[rows, (8 + s) * LANES : (9 + s) * LANES] = (
+            item - top.astype(jnp.float32)
+        ).astype(jnp.bfloat16)
+
+    def forward(c, carry, late):
         trans, red, green, blue = carry
-        power = table(l, 0) + height * (table(l, 1) + height * table(l, 2))
-        alpha = jnp.exp2(power)
-        weight = alpha * trans
-        where = pl.ds(pl.multiple_of(l * 8, 8), 8)
-        alpha_s[where, :] = alpha
-        weight_s[where, :] = weight
-        return (
-            trans * (1.0 - alpha),
-            red + weight * table(l, 3),
-            green + weight * table(l, 4),
-            blue + weight * table(l, 5),
-        )
+        for i in range(16):
+            l = c * 16 + i
+            power = table(l, 0) + height * (table(l, 1) + height * table(l, 2))
+            alpha = jnp.exp2(power)
+            weight = alpha * trans
+            where = pl.ds(pl.multiple_of(l * 8, 8), 8)
+            alpha_s[where, :] = alpha
+            weight_s[where, :] = weight
+            trans = trans * (1.0 - alpha)
+            red = red + weight * table(l, 3)
+            green = green + weight * table(l, 4)
+            blue = blue + weight * table(l, 5)
+            if late and i % 2:
+                relay(weight_s, joint_w, c - 1, i // 2)
+        return trans, red, green, blue
 
     zero = jnp.zeros((8, LANES), jnp.float32)
-    _, red, green, blue = lax.fori_loop(
-        0, entries, forward, (jnp.ones((8, LANES), jnp.float32), zero, zero, zero), unroll=16
-    )
+    chunks = entries // 16
+    carry = forward(0, (jnp.ones((8, LANES), jnp.float32), zero, zero, zero), False)
+    carry = lax.fori_loop(1, chunks, lambda c, v: forward(c, v, True), carry, unroll=UNROLL)
+    red, green, blue = carry[1:]
+    for s in range(8):
+        relay(weight_s, joint_w, chunks - 1, s)
     errors = [2.0 * (item - wanted[8 * k : 8 * k + 8, :]) for k, item in enumerate((red, green, blue))]
     wanted[0:8, :], wanted[8:16, :], wanted[16:24, :] = errors
     tile, _, _ = pixel_terms()
@@ -640,48 +665,48 @@
             top = row.astype(jnp.bfloat16).astype(jnp.float32)
             tops.append(top)
             lows.append(row - top)
-        tops = jnp.concatenate(tops + lows, axis=0).astype(jnp.bfloat16)
-        start = s * 2 * LANES + LANES
-        slopes[48:96, start : start + LANES] = tops
-        start = start + 16 * LANES
-        slopes[48:72, start : start + LANES] = tops[0:24]
-
-    def backward(i, behind):
-        l = entries - 1 - i
-        where = pl.ds(pl.multiple_of(l * 8, 8), 8)
-        slope = errors[0] * table(l, 3) + errors[1] * table(l, 4) + errors[2] * table(l, 5)
-        above = slope - behind
-        slope_s[where, :] = weight_s[where, :] * above
-        return behind + alpha_s[where, :] * above
-
-    lax.fori_loop(0, entries, backward, zero, unroll=16)
-
-    def relay(c, carry):
-        rows = pl.ds(pl.multiple_of(c * 16, 16), 16)
-        for s in range(8):
-            for part, source in enumerate((slope_s, weight_s)):
-                item = source[pl.ds(c * 128 + s, 16, stride=8), :]
-                top = item.astype(jnp.bfloat16)
-                start = s * 2 * LANES + part * LANES
-                joint[rows, start : start + LANES] = top
-                start = start + 16 * LANES
-                joint[rows, start : start + LANES] = (item - top.astype(jnp.float32)).astype(
-                    jnp.bfloat16
-                )
-        return carry
-
-    lax.fori_loop(0, entries // 16, relay, 0, unroll=2)
-    sums = lax.dot_general(
-        joint[...], slopes[...], (((1,), (1,)), ((), ())), preferred_element_type=jnp.float32
-    )
-    turned = [jnp.transpose(sums[q * LANES : (q + 1) * LANES]) for q in range(quarters)]
+        blank = [jnp.zeros((24, LANES), jnp.float32)]
+        start = s * LANES
+        error_sums[:, start : start + LANES] = jnp.concatenate(tops + lows, axis=0).astype(jnp.bfloat16)
+        start = (8 + s) * LANES
+        error_sums[:, start : start + LANES] = jnp.concatenate(tops + blank, axis=0).astype(jnp.bfloat16)
+
+    def backward(c, behind, late):
+        for i in range(15, -1, -1):
+            l = c * 16 + i
+            where = pl.ds(pl.multiple_of(l * 8, 8), 8)
+            slope = errors[0] * table(l, 3) + errors[1] * table(l, 4) + errors[2] * table(l, 5)
+            alpha = alpha_s[where, :]
+            slope_s[where, :] = weight_s[where, :] * (slope - behind)
+            behind = (1.0 - alpha) * behind + alpha * slope
+            if late and i % 2:
+                relay(slope_s, joint_g, c + 1, i // 2)
+        return behind
+
+    behind = backward(chunks - 1, zero, False)
+    lax.fori_loop(
+        1, chunks, lambda i, v: backward(chunks - 1 - i, v, True), behind, unroll=UNROLL
+    )
+    for s in range(8):
+        relay(slope_s, joint_g, 0, s)
+    over = (((1,), (1,)), ((), ()))
+    turned = lax.dot_general(
+        plan_sums[...], joint_g[...], over, preferred_element_type=jnp.float32
+    )
+    tinted = lax.dot_general(
+        error_sums[...], joint_w[...], over, preferred_element_type=jnp.float32
+    )
     for p in range(quarters // 2):
         off_col = moved[16 * p : 16 * p + 8, :]
         off_row = moved[16 * p + 8 : 16 * p + 16, :]
 
         def quantity(j):
-            span = slice(8 * j, 8 * j + 8)
-            return jnp.where(sub < 4, turned[2 * p][span], turned[2 * p + 1][span])
+            source, r = (turned, j) if j < 6 else (tinted, j - 6)
+            rows = source[8 * r : 8 * r + 8]
+            start = 2 * p * LANES
+            return jnp.where(
+                sub < 4, rows[:, start : start + LANES], rows[:, start + LANES : start + 2 * LANES]
+            )
 
         plain, across, down = quantity(0), quantity(1), quantity(2)
         near_col = across - off_col * plain
@@ -714,10 +739,10 @@
 
 
 def main_kernel(
-    params_ref, cam_ref, plan_ref, visible_ref, lists_ref, target_ref, out_ref,
-    held, dense, table, last, plan_order, outgoing, incoming, back, returned, mine, extra, extras, shared,
-    order, wanted, basis, coefs, tables, alpha_s, weight_s, slope_s, joint, slopes, moved, pairs,
-    lhs, hot, own_lhs, own_hot,
+    params_in, cam_in, plan_in, visible_in, lists_in, target_in, out_ref,
+    params_ref, cam_ref, plan_ref, visible_ref, lists_ref, target_ref, dense, table, last, plan_order, outgoing, incoming, back, returned, mine, extra, extras, shared,
+    order, wanted, basis, coefs, tables, alpha_s, weight_s, slope_s, joint_g, joint_w,
+    plan_sums, error_sums, moved, pairs, lhs, hot, own_lhs, own_hot,
     send_one, recv_one, send_two, recv_two, send_three, recv_three, send_four, recv_four, local_sem,
 ):
     cells, views = lax.axis_size("cells"), lax.axis_size("views")
@@ -727,8 +752,21 @@
     capacity = plan_ref.shape[1]
     halves = capacity // LANES
     bits = capacity.bit_length() - 1
-    fetch = pltpu.make_async_copy(params_ref, held, local_sem.at[0])
-    fetch.start()
+    fetches = [
+        pltpu.make_async_copy(source, dest, local_sem.at[i])
+        for i, (source, dest) in enumerate(
+            (
+                (params_in, params_ref),
+                (cam_in, cam_ref),
+                (plan_in, plan_ref),
+                (visible_in, visible_ref),
+                (lists_in, lists_ref),
+                (target_in, target_ref),
+            )
+        )
+    ]
+    for fetch in fetches:
+        fetch.start()
     barrier = pltpu.get_barrier_semaphore()
 
     def greet(axis, me, size):
@@ -758,8 +796,7 @@
 
     greet("cells", cell, cells)
     greet("views", view, views)
-    for b in range(blocks):
-        extra[b : b + 1, :] = visible_ref[:, b * LANES : (b + 1) * LANES].astype(jnp.float32)
+    fetches[1].wait()
     turn, centre = camera_terms(cam_ref[...])
     known = [*turn[0], *turn[1], *turn[2], *centre]
     lane = lax.broadcasted_iota(jnp.int32, (8, LANES), 1)
@@ -767,11 +804,15 @@
     for i, item in enumerate(known):
         line = jnp.where(lane == i, jnp.broadcast_to(item, (8, LANES)), line)
     extra[blocks : blocks + 8, :] = line
-    fetch.wait()
-    fill_dense(held, dense)
+    fetches[3].wait()
+    for b in range(blocks):
+        extra[b : b + 1, :] = visible_ref[:, b * LANES : (b + 1) * LANES].astype(jnp.float32)
+    fetches[0].wait()
+    fill_dense(params_ref, dense)
     feat_parts = [
         project_rows(dense_rows(dense, part, count), turn, centre) for part in range(blocks // 8)
     ]
+    fetches[2].wait()
     send_features(feat_parts, plan_ref, outgoing, table, last, plan_order)
     pl.semaphore_wait(barrier, cells + views - 2)
 
@@ -783,12 +824,13 @@
     )
     incoming[cell] = outgoing[cell]
     extras[view] = extra[...]
-    render_setup(lists_ref, target_ref, order, wanted, basis, slopes, hot, bits)
-    for copy in first:
-        copy.wait()
+    fetches[4].wait()
+    fetches[5].wait()
+    render_setup(lists_ref, target_ref, order, wanted, basis, plan_sums, hot, bits)
     render_rest(
-        cells, incoming, order, wanted, back,
-        coefs, tables, basis, alpha_s, weight_s, slope_s, joint, slopes, moved, pairs, lhs, hot, bits,
+        cells, first, incoming, order, wanted, back,
+        coefs, tables, basis, alpha_s, weight_s, slope_s, joint_g, joint_w, plan_sums, error_sums,
+        moved, pairs, lhs, hot, bits,
     )
     second = send_all(
         "cells", cell, cells, lambda p: back.at[p], lambda p: returned.at[p], send_two, recv_two
@@ -917,10 +959,15 @@
     grads = pl.pallas_call(
         main_kernel,
         out_shape=jax.ShapeDtypeStruct((blocks * PAD_ROWS + blocks, LANES), f32),
-        in_specs=[pl.BlockSpec(memory_space=pl.ANY), vmem, vmem, vmem, vmem, vmem],
+        in_specs=[pl.BlockSpec(memory_space=pltpu.HBM)] * 6,
         out_specs=vmem,
         scratch_shapes=[
             pltpu.VMEM((count, block), f32),
+            pltpu.VMEM(cameras.shape, f32),
+            pltpu.VMEM(plan.shape, jnp.int32),
+            pltpu.VMEM(visible.shape, jnp.int32),
+            pltpu.VMEM(lists.shape, jnp.int32),
+            pltpu.VMEM((3, 1, target.shape[2]), f32),
             pltpu.VMEM((blocks * PAD_ROWS, LANES), f32),
             pltpu.VMEM((blocks * 8, LANES), f32),
             pltpu.VMEM((blocks, LANES), f32),
@@ -938,8 +985,10 @@
             pltpu.VMEM((entries * 8, LANES), f32),
             pltpu.VMEM((entries * 8, LANES), f32),
             pltpu.VMEM((entries * 8, LANES), f32),
-            pltpu.VMEM((entries, 32 * LANES), bf16),
-            pltpu.VMEM((LANES, 32 * LANES), bf16),
+            pltpu.VMEM((entries, 16 * LANES), bf16),
+            pltpu.VMEM((entries, 16 * LANES), bf16),
+            pltpu.VMEM((48, 16 * LANES), bf16),
+            pltpu.VMEM((48, 16 * LANES), bf16),
             pltpu.VMEM((entries // LANES * 8, LANES), f32),
             pltpu.VMEM((tiles * entries // LANES * 16, LANES), f32),
             pltpu.VMEM((cells * 32, tiles * entries), bf16),
@@ -948,15 +997,29 @@
             pltpu.VMEM((2 * LANES, slots * LANES), bf16),
             dma((cells - 1,)), dma((cells - 1,)), dma((cells - 1,)), dma((cells - 1,)),
             dma((views - 1,)), dma((views - 1,)), dma((views - 1,)), dma((views - 1,)),
-            dma((1,)),
+            dma((6,)),
         ],
-        compiler_params=pltpu.CompilerParams(collective_id=0, has_side_effects=True),
-    )(params, cameras, plan, visible, lists, jnp.transpose(target, (1, 0, 2)))
+        compiler_params=pltpu.CompilerParams(
+            collective_id=0, has_side_effects=True, vmem_limit_bytes=MAIN_VMEM
+        ),
+        cost_estimate=pl.CostEstimate(
+            flops=4096 * tiles * 256 * entries,
+            bytes_accessed=4 * count * block,
+            transcendentals=tiles * 256 * entries,
+        ),
+    )(
+        *[
+            pltpu.with_memory_space_constraint(item, pltpu.HBM)
+            for item in (params, cameras, plan, visible, lists, jnp.transpose(target, (1, 0, 2)))
+        ]
+    )
     like = jax.ShapeDtypeStruct(params.shape, f32)
     return tuple(
-        pl.pallas_call(update_kernel, out_shape=(like, like, like))(
-            params, first_moment, second_moment, grads
-        )
+        pl.pallas_call(
+            update_kernel,
+            out_shape=(like, like, like),
+            compiler_params=pltpu.CompilerParams(vmem_limit_bytes=UPDATE_VMEM),
+        )(params, first_moment, second_moment, grads)
     )
 
 

time: 33.8 us -> 29.9 us (0.88)
  Pallas kernels: 32.9 us -> 29.1 us
    pallas_call x1, Pallas kernels: 29.8 us -> 27.5 us  [fused_shards(): pl.pallas_call(main_kernel, out_shape=jax.ShapeDtypeStruct((blocks * PAD_...]
    pallas_call x1, Pallas kernels: 3.07 us -> 1.58 us  [fused_shards(): pl.pallas_call(update_kernel, out_shape=(like, like, like), compiler_para...]
where the time goes in v3:
time: 29.9 us; the launch traced here: 29.8 us
  Pallas kernels  29.1 us (97%)
  between operations  0.69 us (2%)
    pallas_call x1, Pallas kernels, fused_shards(): pl.pallas_call(main_kernel, out_shape=jax.ShapeDtypeStruct((blocks * PAD_...  27.5 us
    pallas_call x1, Pallas kernels, fused_shards(): pl.pallas_call(update_kernel, out_shape=(like, like, like), compiler_para...  1.58 us

profile of v3, /device:TPU:1, one launch (start us, length us, event | category | flops | bytes accessed | tf_op | source)
XLA Modules:
  0.0 29.8 jit_solution(17239310222942794418)
XLA Ops:
  0.6 0.0 copy-start
  0.6 0.0 copy-start.1
  0.7 0.0 copy-start.2
  0.7 27.5 %shard_map.103.grads_ref = f32[1040,128]{1,0:T(8,128)S(1)} custom-call(f32[59,2048]{1,0:T(8,128)} %params_ref.1, f32[1,6]{1,0:T(1,128)} %cam_in.1, s32[8,256]{1,0:T(8,128)} %bitcast.4, s32[1,2048]{1,0:T(1,128)} %visible_in.1, s32[4,512]{1,0:T(4,128)} %bitcast.5, f32[3,1,1024]{2,1,0:T(1,128)} %bitcast.3), custom_call_target="tpu_custom_call" | custom-call | flops 2147483648 | bytes 483328 | tf_op jit(solution)/shard_map/pallas_call | solution.py:959
  28.2 0.0 copy-done
  28.2 0.0 copy-done.1
  28.2 0.0 copy-done.2
  28.2 1.6 %shard_map.104 = (f32[59,2048]{1,0:T(8,128)}, f32[59,2048]{1,0:T(8,128)}, f32[59,2048]{1,0:T(8,128)}) custom-call(f32[59,2048]{1,0:T(8,128)S(1)} %copy-done, f32[59,2048]{1,0:T(8,128)S(1)} %copy-done.1, f32[59,2048]{1,0:T(8,128)S(1)} %copy-done.2, f32[1040,128]{1,0:T(8,128)S(1)} %shard_map.103.grads_ref), custom_call_target="tpu_custom_call" | custom-call | tf_op jit(solution)/shard_map/pallas_call | solution.py:1018
Async XLA Ops:
  0.6 27.5 %copy-start = (f32[59,2048]{1,0:T(8,128)S(1)}, f32[59,2048]{1,0:T(8,128)}, u32[]{:S(2)}) copy-start(f32[59,2048]{1,0:T(8,128)} %params_ref.1) | copy-start | bytes 1449988
  0.6 27.5 %copy-start.1 = (f32[59,2048]{1,0:T(8,128)S(1)}, f32[59,2048]{1,0:T(8,128)}, u32[]{:S(2)}) copy-start(f32[59,2048]{1,0:T(8,128)} %first_ref.1) | copy-start | bytes 1449988
  0.7 27.5 %copy-start.2 = (f32[59,2048]{1,0:T(8,128)S(1)}, f32[59,2048]{1,0:T(8,128)}, u32[]{:S(2)}) copy-start(f32[59,2048]{1,0:T(8,128)} %second_ref.1) | copy-start | bytes 1449988

commit v4 on v3

--- a/solution.py
+++ b/solution.py
@@ -384,7 +384,6 @@
 
 MAIN_VMEM = 40 * 2**20
 UPDATE_VMEM = 16 * 2**20
-UNROLL = 1
 
 
 def fill_dense(params_ref, dense):
@@ -399,7 +398,7 @@
 
 def dense_rows(dense, part, count):
     return [
-        dense[pl.ds(pl.multiple_of((part * PAD_ROWS + r) * 8, 8), 8), :] for r in range(count)
+        dense[(part * PAD_ROWS + r) * 8 : (part * PAD_ROWS + r) * 8 + 8, :] for r in range(count)
     ]
 
 
@@ -429,28 +428,46 @@
     hot[:, start : start + LANES] = jnp.where(row_ids == low, 1.0, 0.0).astype(jnp.bfloat16)
 
 
+def split_two(x):
+    first = x.astype(jnp.bfloat16).astype(jnp.float32)
+    return first, x - first
+
+
 def fill_values(lhs, main, last, index, start, bits):
-    parts = jnp.concatenate(
-        [*split_three(main), *split_three(last), jnp.zeros((5, LANES), jnp.float32)], axis=0
-    )
-    high = jnp.broadcast_to(index >> bits, parts.shape)
-    for b in range(lhs.shape[0] // 32):
-        lhs[32 * b : 32 * b + 32, pl.ds(start, LANES)] = jnp.where(high == b, parts, 0.0).astype(
-            jnp.bfloat16
-        )
-
-
-def scatter_finish(lhs, hot):
-    out = lax.dot_general(
-        lhs[...], hot[...], (((1,), (1,)), ((), ())), preferred_element_type=jnp.float32
-    )
-    pieces = []
-    for b in range(lhs.shape[0] // 32):
-        rows = out[32 * b : 32 * b + 32]
-        pieces.append(
-            (rows[0:8] + rows[8:16] + rows[16:24], rows[24:25] + rows[25:26] + rows[26:27])
-        )
-    return pieces
+    groups = lhs.shape[0] // 18
+    span = slice(start, start + LANES)
+    parts = jnp.concatenate(split_two(main), axis=0)
+    tips = [jnp.broadcast_to(item, (8, LANES)) for item in split_two(last)]
+    high = jnp.broadcast_to(index >> bits, (16, LANES))
+    sub = lax.broadcasted_iota(jnp.int32, (8, LANES), 0)
+    for b in range(groups):
+        lhs[16 * b : 16 * b + 16, span] = jnp.where(high == b, parts, 0.0).astype(jnp.bfloat16)
+    for g in range(groups // 8):
+        here = high[0:8] == sub + 8 * g
+        rows = jnp.concatenate([jnp.where(here, item, 0.0) for item in tips], axis=0)
+        row = 16 * groups + 16 * g
+        lhs[row : row + 16, span] = rows.astype(jnp.bfloat16)
+
+
+def scatter_dot(lhs, hot, rows):
+    return lax.dot_general(
+        lhs[rows], hot[...], (((1,), (1,)), ((), ())), preferred_element_type=jnp.float32
+    )
+
+
+def scatter_main(lhs, hot, first, last):
+    out = scatter_dot(lhs, hot, slice(16 * first, 16 * last))
+    return [out[16 * b : 16 * b + 8] + out[16 * b + 8 : 16 * b + 16] for b in range(last - first)]
+
+
+def scatter_tips(lhs, hot):
+    groups = lhs.shape[0] // 18
+    out = scatter_dot(lhs, hot, slice(16 * groups, 18 * groups))
+    return [
+        out[16 * (b // 8) + b % 8 : 16 * (b // 8) + b % 8 + 1]
+        + out[16 * (b // 8) + 8 + b % 8 : 16 * (b // 8) + 9 + b % 8]
+        for b in range(groups)
+    ]
 
 
 def send_features(feat_parts, plan_ref, out_ref, table, last, order):
@@ -535,7 +552,7 @@
 def render_rest(
     cells, copies, recv_ref, order, wanted, back_ref,
     coefs, tables, basis, alpha_s, weight_s, slope_s, joint_g, joint_w, plan_sums, error_sums,
-    moved, pairs, lhs, hot, bits,
+    turned, tinted, moved, pairs, lhs, hot, bits,
 ):
     owners, packed, _ = recv_ref.shape
     halves = packed // FEATS
@@ -609,8 +626,8 @@
     weights = basis[...].astype(jnp.bfloat16)
     for q in range(quarters):
         span = slice(q * LANES, (q + 1) * LANES)
-        turned = jnp.transpose(coefs[span, :]).astype(jnp.bfloat16)
-        result = jnp.dot(turned, weights, preferred_element_type=jnp.float32)
+        columns = jnp.transpose(coefs[span, :]).astype(jnp.bfloat16)
+        result = jnp.dot(columns, weights, preferred_element_type=jnp.float32)
         for j in range(6):
             tables[j, span, :] = result[:, j * LANES : (j + 1) * LANES]
 
@@ -619,40 +636,45 @@
     def table(l, j):
         return jnp.broadcast_to(tables[j, pl.ds(l, 1), :], (8, LANES))
 
-    def relay(source, joint, c, s):
-        item = source[pl.ds(c * 128 + s, 16, stride=8), :]
+    def relay(source, base, joint, q, c, s):
+        item = source[pl.ds(base + c * 128 + s, 16, stride=8), :]
         top = item.astype(jnp.bfloat16)
-        rows = pl.ds(pl.multiple_of(c * 16, 16), 16)
+        rows = pl.ds(pl.multiple_of(q * LANES, LANES) + c * 16, 16)
         joint[rows, s * LANES : (s + 1) * LANES] = top
         joint[rows, (8 + s) * LANES : (9 + s) * LANES] = (
             item - top.astype(jnp.float32)
         ).astype(jnp.bfloat16)
 
-    def forward(c, carry, late):
+    chunks = LANES // 16
+
+    def forward(q, carry):
         trans, red, green, blue = carry
-        for i in range(16):
-            l = c * 16 + i
-            power = table(l, 0) + height * (table(l, 1) + height * table(l, 2))
-            alpha = jnp.exp2(power)
-            weight = alpha * trans
-            where = pl.ds(pl.multiple_of(l * 8, 8), 8)
-            alpha_s[where, :] = alpha
-            weight_s[where, :] = weight
-            trans = trans * (1.0 - alpha)
-            red = red + weight * table(l, 3)
-            green = green + weight * table(l, 4)
-            blue = blue + weight * table(l, 5)
-            if late and i % 2:
-                relay(weight_s, joint_w, c - 1, i // 2)
+        base = pl.multiple_of(q * 8 * LANES, 8 * LANES)
+        first = pl.multiple_of(q * LANES, LANES)
+        for c in range(chunks):
+            for i in range(16):
+                l = first + (c * 16 + i)
+                where = pl.ds(base + (c * 16 + i) * 8, 8)
+                power = table(l, 0) + height * (table(l, 1) + height * table(l, 2))
+                alpha = jnp.exp2(power)
+                weight = alpha * trans
+                alpha_s[where, :] = alpha
+                weight_s[where, :] = weight
+                trans = trans * (1.0 - alpha)
+                red = red + weight * table(l, 3)
+                green = green + weight * table(l, 4)
+                blue = blue + weight * table(l, 5)
+                if c and i % 2:
+                    relay(weight_s, base, joint_w, q, c - 1, i // 2)
+        for s in range(8):
+            relay(weight_s, base, joint_w, q, chunks - 1, s)
         return trans, red, green, blue
 
     zero = jnp.zeros((8, LANES), jnp.float32)
-    chunks = entries // 16
-    carry = forward(0, (jnp.ones((8, LANES), jnp.float32), zero, zero, zero), False)
-    carry = lax.fori_loop(1, chunks, lambda c, v: forward(c, v, True), carry, unroll=UNROLL)
+    carry = lax.fori_loop(
+        0, quarters, forward, (jnp.ones((8, LANES), jnp.float32), zero, zero, zero)
+    )
     red, green, blue = carry[1:]
-    for s in range(8):
-        relay(weight_s, joint_w, chunks - 1, s)
     errors = [2.0 * (item - wanted[8 * k : 8 * k + 8, :]) for k, item in enumerate((red, green, blue))]
     wanted[0:8, :], wanted[8:16, :], wanted[16:24, :] = errors
     tile, _, _ = pixel_terms()
@@ -671,41 +693,52 @@
         start = (8 + s) * LANES
         error_sums[:, start : start + LANES] = jnp.concatenate(tops + blank, axis=0).astype(jnp.bfloat16)
 
-    def backward(c, behind, late):
-        for i in range(15, -1, -1):
-            l = c * 16 + i
-            where = pl.ds(pl.multiple_of(l * 8, 8), 8)
-            slope = errors[0] * table(l, 3) + errors[1] * table(l, 4) + errors[2] * table(l, 5)
-            alpha = alpha_s[where, :]
-            slope_s[where, :] = weight_s[where, :] * (slope - behind)
-            behind = (1.0 - alpha) * behind + alpha * slope
-            if late and i % 2:
-                relay(slope_s, joint_g, c + 1, i // 2)
+    def sum_pixels(factors, joint, result, q):
+        span = pl.ds(pl.multiple_of(q * LANES, LANES), LANES)
+        result[:, span] = lax.dot_general(
+            factors[...],
+            joint[span, :],
+            (((1,), (1,)), ((), ())),
+            preferred_element_type=jnp.float32,
+        )
+
+    def backward(q, behind, late):
+        base = pl.multiple_of(q * 8 * LANES, 8 * LANES)
+        first = pl.multiple_of(q * LANES, LANES)
+        sum_pixels(error_sums, joint_w, tinted, q)
+        if late:
+            sum_pixels(plan_sums, joint_g, turned, q + 1)
+        for c in range(chunks - 1, -1, -1):
+            for i in range(15, -1, -1):
+                l = first + (c * 16 + i)
+                where = pl.ds(base + (c * 16 + i) * 8, 8)
+                slope = errors[0] * table(l, 3) + errors[1] * table(l, 4) + errors[2] * table(l, 5)
+                alpha = alpha_s[where, :]
+                slope_s[(c * 16 + i) * 8 : (c * 16 + i) * 8 + 8, :] = weight_s[where, :] * (
+                    slope - behind
+                )
+                behind = (1.0 - alpha) * behind + alpha * slope
+                if c < chunks - 1 and i % 2:
+                    relay(slope_s, 0, joint_g, q, c + 1, i // 2)
+        for s in range(8):
+            relay(slope_s, 0, joint_g, q, 0, s)
         return behind
 
-    behind = backward(chunks - 1, zero, False)
-    lax.fori_loop(
-        1, chunks, lambda i, v: backward(chunks - 1 - i, v, True), behind, unroll=UNROLL
-    )
-    for s in range(8):
-        relay(slope_s, joint_g, 0, s)
-    over = (((1,), (1,)), ((), ()))
-    turned = lax.dot_general(
-        plan_sums[...], joint_g[...], over, preferred_element_type=jnp.float32
-    )
-    tinted = lax.dot_general(
-        error_sums[...], joint_w[...], over, preferred_element_type=jnp.float32
-    )
+    behind = backward(quarters - 1, zero, False)
+    lax.fori_loop(1, quarters, lambda i, v: backward(quarters - 1 - i, v, True), behind)
+    sum_pixels(plan_sums, joint_g, turned, 0)
     for p in range(quarters // 2):
         off_col = moved[16 * p : 16 * p + 8, :]
         off_row = moved[16 * p + 8 : 16 * p + 16, :]
 
         def quantity(j):
             source, r = (turned, j) if j < 6 else (tinted, j - 6)
-            rows = source[8 * r : 8 * r + 8]
+            rows = slice(8 * r, 8 * r + 8)
             start = 2 * p * LANES
             return jnp.where(
-                sub < 4, rows[:, start : start + LANES], rows[:, start + LANES : start + 2 * LANES]
+                sub < 4,
+                source[rows, start : start + LANES],
+                source[rows, start + LANES : start + 2 * LANES],
             )
 
         plain, across, down = quantity(0), quantity(1), quantity(2)
@@ -731,7 +764,7 @@
             o * LANES,
             bits,
         )
-    for s, (main, last) in enumerate(scatter_finish(lhs, hot)):
+    for s, (main, last) in enumerate(zip(scatter_main(lhs, hot, 0, owners), scatter_tips(lhs, hot))):
         for h in range(halves):
             span = slice(h * LANES, (h + 1) * LANES)
             back_ref[s, 8 * h : 8 * h + 8, :] = main[:, span]
@@ -742,7 +775,7 @@
     params_in, cam_in, plan_in, visible_in, lists_in, target_in, out_ref,
     params_ref, cam_ref, plan_ref, visible_ref, lists_ref, target_ref, dense, table, last, plan_order, outgoing, incoming, back, returned, mine, extra, extras, shared,
     order, wanted, basis, coefs, tables, alpha_s, weight_s, slope_s, joint_g, joint_w,
-    plan_sums, error_sums, moved, pairs, lhs, hot, own_lhs, own_hot,
+    plan_sums, error_sums, turned, tinted, moved, pairs, lhs, hot, own_lhs, own_hot,
     send_one, recv_one, send_two, recv_two, send_three, recv_three, send_four, recv_four, local_sem,
 ):
     cells, views = lax.axis_size("cells"), lax.axis_size("views")
@@ -830,37 +863,48 @@
     render_rest(
         cells, first, incoming, order, wanted, back,
         coefs, tables, basis, alpha_s, weight_s, slope_s, joint_g, joint_w, plan_sums, error_sums,
-        moved, pairs, lhs, hot, bits,
+        turned, tinted, moved, pairs, lhs, hot, bits,
     )
     second = send_all(
         "cells", cell, cells, lambda p: back.at[p], lambda p: returned.at[p], send_two, recv_two
     )
     returned[cell] = back[cell]
     wide = own_hot.shape[0].bit_length() - 1
-    for o in range(cells * halves):
-        d, h = divmod(o, halves)
-        fill_hot(own_hot, plan_ref[d : d + 1, h * LANES : (h + 1) * LANES], o * LANES, wide)
-    for copy in second:
-        copy.wait()
-    for o in range(cells * halves):
-        d, h = divmod(o, halves)
+    spots = []
+    for k in range(cells):
+        origin = lax.rem(cell + cells - k, cells)
+        for h in range(halves):
+            row = plan_order[pl.ds(origin * halves + h, 1), :]
+            fill_hot(own_hot, row, (k * halves + h) * LANES, wide)
+            spots.append((k, h, origin, row))
+    for k, h, origin, row in spots:
+        if k and h == 0:
+            second[k - 1].wait()
         fill_values(
             own_lhs,
-            returned[d, 8 * h : 8 * h + 8, :],
-            returned[d, 8 * halves + h : 8 * halves + h + 1, :],
-            plan_ref[d : d + 1, h * LANES : (h + 1) * LANES],
-            o * LANES,
+            returned[origin, 8 * h : 8 * h + 8, :],
+            returned[origin, 8 * halves + h : 8 * halves + h + 1, :],
+            row,
+            (k * halves + h) * LANES,
             wide,
         )
-    for g, (main, tip) in enumerate(scatter_finish(own_lhs, own_hot)):
-        for i in range(2):
-            span = slice(i * LANES, (i + 1) * LANES)
-            for f in range(8):
-                mine[f * blocks + 2 * g + i : f * blocks + 2 * g + i + 1, :] = main[f : f + 1, span]
-            mine[8 * blocks + 2 * g + i : 8 * blocks + 2 * g + i + 1, :] = tip[:, span]
-    third = send_all(
-        "views", view, views, lambda p: mine, lambda p: shared.at[p], send_three, recv_three
-    )
+    tips = scatter_tips(own_lhs, own_hot)
+    parts = blocks // 8
+    third = []
+    for part in range(parts):
+        for g, main in enumerate(scatter_main(own_lhs, own_hot, 4 * part, 4 * part + 4)):
+            for i in range(2):
+                span = slice(i * LANES, (i + 1) * LANES)
+                for f in range(8):
+                    mine[part, f * 8 + 2 * g + i : f * 8 + 2 * g + i + 1, :] = main[f : f + 1, span]
+                mine[part, 64 + 2 * g + i : 64 + 2 * g + i + 1, :] = tips[4 * part + g][:, span]
+        third.append(
+            send_all(
+                "views", view, views,
+                lambda p: mine.at[part], lambda p: shared.at[p, part],
+                send_three.at[part], recv_three.at[part],
+            )
+        )
     for copy in fourth:
         copy.wait()
     counts = extras[0, 0:blocks, :]
@@ -869,18 +913,15 @@
     grads = blocks * PAD_ROWS
     out_ref[grads : grads + blocks, :] = counts
 
-    def pull_view(fresh, source, lines):
+    def pull_view(fresh, part, source, lines):
         known = [jnp.broadcast_to(lines[:, i : i + 1], (8, LANES)) for i in range(12)]
         turn = [known[0:3], known[3:6], known[6:9]]
         centre = known[9:12]
-
-        def one_part(part, carry):
-            rows = dense_rows(dense, part, count)
-            feats, pull = jax.vjp(lambda *items: project_rows(items, turn, centre), *rows)
-            got = [
-                source[pl.ds(pl.multiple_of(f * blocks + part * 8, 8), 8), :] for f in range(FEATS)
-            ]
-            wanted_slopes = (
+        rows = dense_rows(dense, part, count)
+        feats, pull = jax.vjp(lambda *items: project_rows(items, turn, centre), *rows)
+        got = [source[8 * f : 8 * f + 8, :] for f in range(FEATS)]
+        pulled = pull(
+            (
                 feats[2] * got[1] + feats[3] * got[2],
                 feats[3] * got[1] + feats[4] * got[2],
                 -0.5 * got[3],
@@ -891,18 +932,18 @@
                 got[7],
                 got[8],
             )
-            for r, item in enumerate(pull(wanted_slopes)):
-                where = pl.ds(pl.multiple_of((part * PAD_ROWS + r) * 8, 8), 8)
-                out_ref[where, :] = item if fresh else out_ref[where, :] + item
-            return carry
-
-        lax.fori_loop(0, blocks // 8, one_part, 0)
-
-    pull_view(True, mine, extra[blocks : blocks + 1, :])
-    for k in range(1, views):
-        third[views - 1 - k].wait()
-        origin = lax.rem(view + k, views)
-        pull_view(False, shared.at[origin], extras[origin, blocks : blocks + 1, :])
+        )
+        for r, item in enumerate(pulled):
+            where = slice((part * PAD_ROWS + r) * 8, (part * PAD_ROWS + r) * 8 + 8)
+            out_ref[where, :] = item if fresh else out_ref[where, :] + item
+
+    for part in range(parts):
+        pull_view(True, part, mine.at[part], extra[blocks : blocks + 1, :])
+    for part in range(parts):
+        for k in range(1, views):
+            third[part][views - 1 - k].wait()
+            origin = lax.rem(view + k, views)
+            pull_view(False, part, shared.at[origin, part], extras[origin, blocks : blocks + 1, :])
 
 
 def update_kernel(params_ref, first_ref, second_ref, grads_ref, new_ref, new_first_ref, new_second_ref):
@@ -973,10 +1014,10 @@
             pltpu.VMEM((blocks, LANES), f32),
             pltpu.VMEM((slots, LANES), jnp.int32),
             packet, packet, packet, packet,
-            pltpu.VMEM((FEATS * blocks, LANES), f32),
+            pltpu.VMEM((blocks // 8, FEATS * 8, LANES), f32),
             pltpu.VMEM((blocks + 8, LANES), f32),
             pltpu.VMEM((views, blocks + 8, LANES), f32),
-            pltpu.VMEM((views, FEATS * blocks, LANES), f32),
+            pltpu.VMEM((views, blocks // 8, FEATS * 8, LANES), f32),
             pltpu.VMEM((tiles * entries // LANES, LANES), jnp.int32),
             pltpu.VMEM((24, LANES), f32),
             pltpu.VMEM((LANES, 6 * LANES), f32),
@@ -984,19 +1025,21 @@
             pltpu.VMEM((6, entries, LANES), f32),
             pltpu.VMEM((entries * 8, LANES), f32),
             pltpu.VMEM((entries * 8, LANES), f32),
-            pltpu.VMEM((entries * 8, LANES), f32),
+            pltpu.VMEM((8 * LANES, LANES), f32),
             pltpu.VMEM((entries, 16 * LANES), bf16),
             pltpu.VMEM((entries, 16 * LANES), bf16),
             pltpu.VMEM((48, 16 * LANES), bf16),
             pltpu.VMEM((48, 16 * LANES), bf16),
+            pltpu.VMEM((48, entries), f32),
+            pltpu.VMEM((48, entries), f32),
             pltpu.VMEM((entries // LANES * 8, LANES), f32),
             pltpu.VMEM((tiles * entries // LANES * 16, LANES), f32),
-            pltpu.VMEM((cells * 32, tiles * entries), bf16),
+            pltpu.VMEM((cells * 18, tiles * entries), bf16),
             pltpu.VMEM((capacity, tiles * entries), bf16),
-            pltpu.VMEM((blocks // 2 * 32, slots * LANES), bf16),
+            pltpu.VMEM((blocks // 2 * 18, slots * LANES), bf16),
             pltpu.VMEM((2 * LANES, slots * LANES), bf16),
             dma((cells - 1,)), dma((cells - 1,)), dma((cells - 1,)), dma((cells - 1,)),
-            dma((views - 1,)), dma((views - 1,)), dma((views - 1,)), dma((views - 1,)),
+            dma((blocks // 8, views - 1)), dma((blocks // 8, views - 1)), dma((views - 1,)), dma((views - 1,)),
             dma((6,)),
         ],
         compiler_params=pltpu.CompilerParams(
@@ -1029,10 +1072,10 @@
     halves = capacity // LANES
     fits = (
         capacity % LANES == 0
-        and params.shape[1] % (8 * LANES) == 0
+        and params.shape[1] % (16 * LANES) == 0
         and entries % (2 * LANES) == 0
         and 8 % max(halves, 1) == 0
-        and lax.axis_size("cells") * halves % 8 == 0
+        and lax.axis_size("cells") % 8 == 0
         and tiles * entries <= 4096
         and tiles == 4
     )

time: 29.9 us -> 29.3 us (0.980)
  Pallas kernels: 29.1 us -> 28.4 us
    pallas_call x1, Pallas kernels: 27.5 us -> 26.8 us  [fused_shards(): pl.pallas_call(main_kernel, out_shape=jax.ShapeDtypeStruct((blocks * PAD_...]
where the time goes in v4:
time: 29.3 us; the launch traced here: 29.1 us
  Pallas kernels  28.4 us (97%)
  between operations  0.69 us (2%)
    pallas_call x1, Pallas kernels, fused_shards(): pl.pallas_call(main_kernel, out_shape=jax.ShapeDtypeStruct((blocks * PAD_...  26.8 us
    pallas_call x1, Pallas kernels, fused_shards(): pl.pallas_call(update_kernel, out_shape=(like, like, like), compiler_para...  1.58 us

profile of v4, /device:TPU:1, one launch (start us, length us, event | category | flops | bytes accessed | tf_op | source)
XLA Modules:
  0.0 29.1 jit_solution(9304558872735125110)
XLA Ops:
  0.6 0.0 copy-start
  0.6 0.0 copy-start.1
  0.7 0.0 copy-start.2
  0.7 26.8 %shard_map.103.grads_ref = f32[1040,128]{1,0:T(8,128)S(1)} custom-call(f32[59,2048]{1,0:T(8,128)} %params_ref.1, f32[1,6]{1,0:T(1,128)} %cam_in.1, s32[8,256]{1,0:T(8,128)} %bitcast.4, s32[1,2048]{1,0:T(1,128)} %visible_in.1, s32[4,512]{1,0:T(4,128)} %bitcast.5, f32[3,1,1024]{2,1,0:T(1,128)} %bitcast.3), custom_call_target="tpu_custom_call" | custom-call | flops 2147483648 | bytes 483328 | tf_op jit(solution)/shard_map/pallas_call | solution.py:1000
  27.5 0.0 copy-done
  27.5 0.0 copy-done.1
  27.5 0.0 copy-done.2
  27.5 1.6 %shard_map.104 = (f32[59,2048]{1,0:T(8,128)}, f32[59,2048]{1,0:T(8,128)}, f32[59,2048]{1,0:T(8,128)}) custom-call(f32[59,2048]{1,0:T(8,128)S(1)} %copy-done, f32[59,2048]{1,0:T(8,128)S(1)} %copy-done.1, f32[59,2048]{1,0:T(8,128)S(1)} %copy-done.2, f32[1040,128]{1,0:T(8,128)S(1)} %shard_map.103.grads_ref), custom_call_target="tpu_custom_call" | custom-call | tf_op jit(solution)/shard_map/pallas_call | solution.py:1061
Async XLA Ops:
  0.6 26.9 %copy-start = (f32[59,2048]{1,0:T(8,128)S(1)}, f32[59,2048]{1,0:T(8,128)}, u32[]{:S(2)}) copy-start(f32[59,2048]{1,0:T(8,128)} %params_ref.1) | copy-start | bytes 1449988
  0.6 26.9 %copy-start.1 = (f32[59,2048]{1,0:T(8,128)S(1)}, f32[59,2048]{1,0:T(8,128)}, u32[]{:S(2)}) copy-start(f32[59,2048]{1,0:T(8,128)} %first_ref.1) | copy-start | bytes 1449988
  0.7 26.9 %copy-start.2 = (f32[59,2048]{1,0:T(8,128)S(1)}, f32[59,2048]{1,0:T(8,128)}, u32[]{:S(2)}) copy-start(f32[59,2048]{1,0:T(8,128)} %second_ref.1) | copy-start | bytes 1449988
